TPU v7x, 256 devices: a whole 4x4x8 slice. The times are simulated.
256 devices in a mesh: gy: 16 (over y_lo, x, core), gx: 16 (over y_hi, z).
Axes of the slice: x: 4, y: 4 (y_hi: 2, y_lo: 2; y = y_hi * 2 + y_lo), z: 8, core: 2. Of those that a mesh axis runs over, the one named last changes fastest.
Arguments:
- tracer: float32 [8, 2048, 4096], P(None, 'gy', 'gx'), may hold values from -6 to 6
- east_speed: float32 [8, 2048, 4096], P(None, 'gy', 'gx'), may hold values from -0.25 to 0.25
- north_speed: float32 [8, 2048, 4096], P(None, 'gy', 'gx'), may hold values from -0.25 to 0.25
- columns: int32 [2048, 4096], P('gy', 'gx'), may hold values from 0 to 8
- thickness: float32 [8], replicated, may hold values from 0.5 to 2
- surface_flux: float32 [2048, 4096], P('gy', 'gx'), may hold values from -6 to 6
- helm: float32 [2048, 4096], P('gy', 'gx'), may hold values from 0.2 to 4
Outputs:
- tracer_new: float32 [8, 2048, 4096], P(None, 'gy', 'gx')
- heights: float32 [2048, 4096], P('gy', 'gx')
Inputs may be any that keep to these rules, and one draw needn't show every extreme that they name: `columns`: ocean levels per column; 0 means land.
All inputs are finite; a program needn't handle non-finite values.
Results may differ from a plain program's by a relative error of at most 0.0001.
Values sent between devices are 32-bit elements; how exact they have to be, the bound alone decides.
A program may use at most 64 MiB of HBM per device.

v0:
```python
import functools

import jax
import jax.numpy as jnp
from jax import lax
from jax.sharding import Mesh
from jax.sharding import PartitionSpec as P

TSTEPS = 2
ITERS = 3
GY_GX = ("gy_0", "gy_1", "gy_2", "gx_0", "gx_1")
GY = ("gy_0", "gy_1", "gy_2")
GX = ("gx_0", "gx_1")


def extended_2(array, sides, width):
    for axis, dim in sides:
        peers, length = (lax.axis_size(axis), array.shape[dim])
        up = [(i, (i + 1) % peers) for i in range(peers)]
        down = [(j, i) for i, j in up]
        last = lax.slice_in_dim(array, length - width, length, axis=dim)
        first = lax.slice_in_dim(array, 0, width, axis=dim)
        before = lax.ppermute(last, axis, up)
        after = lax.ppermute(first, axis, down)
        array = jnp.concatenate([before, array, after], axis=dim)
    return array


def over_axes(array, axes):
    return functools.reduce(lax.psum, axes, array)


def upwind(speed, behind, ahead):
    return jnp.maximum(speed, 0.0) * behind + jnp.minimum(speed, 0.0) * ahead


def advect_block(extended, east_ext, north_ext, ocean_ext):
    centre = extended[:, 1:-1, 1:-1]
    open_east = ocean_ext[:, 1:-1, :-1] * ocean_ext[:, 1:-1, 1:]
    flux_east = open_east * upwind(
        east_ext[:, 1:-1, :-1], extended[:, 1:-1, :-1], extended[:, 1:-1, 1:]
    )
    open_north = ocean_ext[:, :-1, 1:-1] * ocean_ext[:, 1:, 1:-1]
    flux_north = open_north * upwind(
        north_ext[:, :-1, 1:-1], extended[:, :-1, 1:-1], extended[:, 1:, 1:-1]
    )
    return centre - (
        flux_east[:, :, 1:] - flux_east[:, :, :-1] + flux_north[:, 1:, :] - flux_north[:, :-1, :]
    )


def stencil(extended, wet_ext, diagonal_term):
    weighted = wet_ext * extended
    edges = weighted[1:-1, 2:] + weighted[1:-1, :-2] + weighted[2:, 1:-1] + weighted[:-2, 1:-1]
    corners = weighted[2:, 2:] + weighted[2:, :-2] + weighted[:-2, 2:] + weighted[:-2, :-2]
    return diagonal_term * extended[1:-1, 1:-1] - wet_ext[1:-1, 1:-1] * (edges + 0.5 * corners)


def solve(forcing, diagonal_term, apply_matrix, sum_all):
    heights = jnp.zeros_like(forcing)
    residual = forcing
    scaled = residual / diagonal_term
    applied = apply_matrix(scaled)
    product_now, curvature = sum_all((jnp.sum(residual * scaled), jnp.sum(applied * scaled)))
    step_size = product_now / curvature
    direction = scaled
    along = applied
    for iteration in range(ITERS):
        heights = heights + step_size * direction
        residual = residual - step_size * along
        if iteration + 1 < ITERS:
            scaled = residual / diagonal_term
            applied = apply_matrix(scaled)
            product_next, curvature = sum_all(
                (jnp.sum(residual * scaled), jnp.sum(applied * scaled))
            )
            factor = product_next / product_now
            step_size = product_next / (curvature - factor * product_next / step_size)
            direction = scaled + factor * direction
            along = applied + factor * along
            product_now = product_next
    return heights


def on_device(tracer, east_speed, north_speed, columns, thickness, surface_flux, helm):
    levels, rows_dev, cols_dev = tracer.shape
    depth = lax.broadcasted_iota(jnp.int32, tracer.shape, 0)
    ocean = (depth < columns[None]).astype(jnp.float32)
    stacked = jnp.stack([east_speed, north_speed, ocean])
    static_ext = extended_2(stacked, ((GY, 2), (GX, 3)), 1)
    position = lax.axis_index(GY)
    last_row = lax.axis_size(GY) - 1
    row_ids = lax.broadcasted_iota(jnp.int32, (rows_dev + 2, 1), 0)
    closed = (row_ids == 0) & (position == 0) | (row_ids == rows_dev + 1) & (position == last_row)
    row_keep = jnp.where(closed, 0.0, 1.0).astype(jnp.float32)
    ocean_ext = static_ext[2] * row_keep[None]
    current = tracer
    for section_index in range(TSTEPS):
        extended = extended_2(current, ((GY, 1), (GX, 2)), 1)
        current = advect_block(extended, static_ext[0], static_ext[1], ocean_ext)
    forcing = surface_flux + jnp.sum(thickness[:, None, None] * ocean * current, axis=0)
    wet_ext = ocean_ext[0]
    diagonal_term = 6.0 + helm

    def apply_grid(source):
        rimmed = extended_2(source, ((GY, 0), (GX, 1)), 1)
        return stencil(rimmed, wet_ext, diagonal_term)

    def sum_grid(values):
        return jax.tree.map(lambda part: over_axes(part, GY_GX), values)

    heights = solve(forcing, diagonal_term, apply_grid, sum_grid)
    return (current, heights)


def solution(mesh):
    split = Mesh(mesh.devices.reshape(2, 4, 2, 2, 8), ("gy_0", "gy_1", "gy_2", "gx_0", "gx_1"))
    in_specs = (
        P(None, GY, GX),
        P(None, GY, GX),
        P(None, GY, GX),
        P(GY, GX),
        P(),
        P(GY, GX),
        P(GY, GX),
    )
    out_specs = (P(None, GY, GX), P(GY, GX))
    return jax.shard_map(
        on_device, mesh=split, in_specs=in_specs, out_specs=out_specs, check_vma=False
    )
```

profile of v0, /device:TPU:1, one launch (start us, length us, event | category | flops | bytes accessed | tf_op | source)
XLA Modules:
  0.0 252.7 jit_solution(864464282848693614)
XLA Ops:
  1.6 2.7 %collective-permute-start.4 = (f32[8,1,256]{2,1,0:T(1,128)S(1)}, f32[8,1,256]{2,1,0:T(1,128)S(1)}, u32[]{:S(2)}, u32[]{:S(2)}) collective-permute-start(f32[8,1,256]{2,1,0:T(1,128)S(1)} %get-tuple-element.61), channel_id=1, source_target_pairs={{0,16},{16,32},{32,48},{48,64},{64,80},{80,96},{96,112},{112,128},... | collective-permute-start | bytes 24584 | tf_op jit(solution)/shard_map/ppermute | solution.py:23
  7.0 1.1 collective-permute-start
  8.1 2.8 %collective-permute-start.1 = (f32[3,8,1,256]{3,2,1,0:T(1,128)S(1)}, f32[3,8,1,256]{3,2,1,0:T(1,128)S(1)}, u32[]{:S(2)}, u32[]{:S(2)}) collective-permute-start(f32[3,8,1,256]{3,2,1,0:T(1,128)S(1)} %get-tuple-element.53), channel_id=1, source_target_pairs={{16,0},{32,16},{48,32},{64,48},{80,64},{96,80},{112,96},{128,112},... | collective-permute-start | bytes 73736 | tf_op jit(solution)/shard_map/ppermute | solution.py:24
  12.0 6.5 %collective-permute-start.7 = (f32[8,130,1]{1,0,2:T(8,128)S(1)}, f32[8,130,1]{1,0,2:T(8,128)S(1)}, u32[]{:S(2)}, u32[]{:S(2)}) collective-permute-start(f32[8,130,1]{1,0,2:T(8,128)S(1)} %copy.29), channel_id=1, source_target_pairs={{1,0},{2,1},{3,2},{4,3},{5,4},{6,5},{7,6},{8,7},{9,8},{10,9},{11,1... | collective-permute-start | bytes 12488 | tf_op jit(solution)/shard_map/ppermute | solution.py:24
  18.6 1.9 pad_maximum_fusion.1
  20.4 2.2 fusion.33
  22.7 2.3 copy.23
  25.1 2.3 copy.24
  27.4 5.3 %collective-permute-start.3 = (f32[3,8,130,1]{2,1,3,0:T(8,128)S(1)}, f32[3,8,130,1]{2,1,3,0:T(8,128)S(1)}, u32[]{:S(2)}, u32[]{:S(2)}) collective-permute-start(f32[3,8,130,1]{2,1,3,0:T(8,128)S(1)} %copy.24), channel_id=1, source_target_pairs={{1,0},{2,1},{3,2},{4,3},{5,4},{6,5},{7,6},{8,7},{9,8},{10,9},{11,1... | collective-permute-start | bytes 37448 | tf_op jit(solution)/shard_map/ppermute | solution.py:24
  33.0 1.1 copy.30
  34.0 1.8 copy.25
  35.8 1.8 copy.26
  37.6 5.7 %pad_maximum_fusion = f32[3,8,130,258]{3,2,1,0:T(8,128)S(1)} fusion(f32[3,8,130,1]{3,2,1,0:T(8,128)} %copy.26, f32[3,8,1,256]{3,2,1,0:T(1,128)S(1)} %collective-permute-done.1, f32[1,8,128,256]{3,2,1,0:T(8,128)S(1)} %fusion.15, f32[1,8,128,256]{3,2,1,0:T(8,128)} %bitcast.19, f32[1,8,128,256]{3,2,1,0:T(8,128)} %bitcast.23, ...), kind=kLoop, calls=%fused_computation | loop fusion | flops 4829760 | bytes 6439680 | tf_op jit(solution)/shard_map/concatenate | solution.py:25
  45.7 1.3 fusion.7
  47.4 1.6 collective-permute-start.8
  48.9 3.2 %collective-permute-start.9 = (f32[8,1,256]{2,1,0:T(1,128)S(1)}, f32[8,1,256]{2,1,0:T(1,128)S(1)}, u32[]{:S(2)}, u32[]{:S(2)}) collective-permute-start(f32[8,1,256]{2,1,0:T(1,128)S(1)} %get-tuple-element.58), channel_id=1, source_target_pairs={{16,0},{32,16},{48,32},{64,48},{80,64},{96,80},{112,96},{128,112},... | collective-permute-start | bytes 24584 | tf_op jit(solution)/shard_map/ppermute | solution.py:24
  54.1 1.4 copy.31
  55.9 5.3 %collective-permute-start.11 = (f32[8,130,1]{1,0,2:T(8,128)S(1)}, f32[8,130,1]{1,0,2:T(8,128)S(1)}, u32[]{:S(2)}, u32[]{:S(2)}) collective-permute-start(f32[8,130,1]{1,0,2:T(8,128)S(1)} %copy.33), channel_id=1, source_target_pairs={{1,0},{2,1},{3,2},{4,3},{5,4},{6,5},{7,6},{8,7},{9,8},{10,9},{11,1... | collective-permute-start | bytes 12488 | tf_op jit(solution)/shard_map/ppermute | solution.py:24
  61.2 3.4 %fusion.12 = f32[8,129,256]{2,1,0:T(8,128)} fusion(f32[8,128,256]{2,1,0:T(8,128)S(1)} %fusion.14, f32[8,1,256]{2,1,0:T(1,128)S(1)} %collective-permute-done.8, f32[8,1,256]{2,1,0:T(1,128)S(1)} %collective-permute-done.9, f32[8,130,258]{2,1,0:T(8,128)} %copy-done.5, f32[8,130,258]{2,1,0:T(8,128)S(1)} %fusion), kind=kLoop, calls=%fused_computation.38 | loop fusion | flops 2377728 | bytes 5292032 | tf_op jit(solution)/shard_map/mul | solution.py:44
  64.9 1.1 copy.34
  65.9 2.8 %fusion.3 = f32[8,128,257]{2,1,0:T(8,128)S(1)} fusion(f32[8,130,1]{2,1,0:T(8,128)} %copy.34, f32[8,1,256]{2,1,0:T(1,128)S(1)} %collective-permute-done.9, f32[8,128,256]{2,1,0:T(8,128)S(1)} %fusion.14, f32[8,1,256]{2,1,0:T(1,128)S(1)} %collective-permute-done.8, f32[8,130,1]{2,1,0:T(8,128)S(1)} %copy.32, f32[8,130,258]{2,1,0:T(8,128)} %copy-done.2, ...), kind=kLoop, calls=%fused_computation.9 | loop fusion | flops 3421184 | bytes 5283968 | tf_op jit(solution)/shard_map/mul | solution.py:40
  68.8 1.5 multiply_reduce_fusion
  70.4 4.9 %collective-permute-start.13 = (f32[1,256]{1,0:T(1,128)S(1)}, f32[1,256]{1,0:T(1,128)S(1)}, u32[]{:S(2)}, u32[]{:S(2)}) collective-permute-start(f32[1,256]{1,0:T(1,128)S(1)} %get-tuple-element.73), channel_id=1, source_target_pairs={{16,0},{32,16},{48,32},{64,48},{80,64},{96,80},{112,96},{128,112},... | collective-permute-start | bytes 3080 | tf_op jit(solution)/shard_map/ppermute | solution.py:24
  76.4 5.1 %collective-permute-start.15 = (f32[130,1]{1,0:T(8,128)S(1)}, f32[130,1]{1,0:T(8,128)S(1)}, u32[]{:S(2)}, u32[]{:S(2)}) collective-permute-start(f32[130,1]{1,0:T(8,128)S(1)} %get-tuple-element.67), channel_id=1, source_target_pairs={{1,0},{2,1},{3,2},{4,3},{5,4},{6,5},{7,6},{8,7},{9,8},{10,9},{11,1... | collective-permute-start | bytes 1568 | tf_op jit(solution)/shard_map/ppermute | solution.py:24
  81.5 1.7 collective-permute-done.14
  84.2 4.5 %all-reduce.14 = (f32[]{:T(128)}, f32[]{:T(128)}) all-reduce(f32[]{:T(128)} %get-tuple-element.9, f32[]{:T(128)} %get-tuple-element.8), channel_id=1, replica_groups=mesh['gy_0'=2,'gy_1'=4,'gy_2'=2,'gx_0'=2,'gx_1'=8] {'gy_0'}, use_global_device_ids=true, to_apply=%region_2.3 | all-reduce | flops 2 | bytes 16 | tf_op jit(solution)/shard_map/psum | solution.py:30
  88.7 13.6 %all-reduce.5 = (f32[]{:T(128)}, f32[]{:T(128)}) all-reduce(f32[]{:T(128)} %get-tuple-element.38, f32[]{:T(128)} %get-tuple-element.39), channel_id=1, replica_groups=mesh['gy_0'=2,'gy_1'=4,'gy_2'=2,'gx_0'=2,'gx_1'=8] {'gy_1'}, use_global_device_ids=true, to_apply=%region_3.4 | all-reduce | flops 2 | bytes 16 | tf_op jit(solution)/shard_map/psum | solution.py:30
  102.3 4.0 %all-reduce.11 = (f32[]{:T(128)}, f32[]{:T(128)}) all-reduce(f32[]{:T(128)} %get-tuple-element.20, f32[]{:T(128)} %get-tuple-element.21), channel_id=1, replica_groups=mesh['gy_0'=2,'gy_1'=4,'gy_2'=2,'gx_0'=2,'gx_1'=8] {'gy_2'}, use_global_device_ids=true, to_apply=%region_4.5 | all-reduce | flops 2 | bytes 16 | tf_op jit(solution)/shard_map/psum | solution.py:30
  106.3 5.9 %all-reduce.8 = (f32[]{:T(128)}, f32[]{:T(128)}) all-reduce(f32[]{:T(128)} %get-tuple-element.32, f32[]{:T(128)} %get-tuple-element.33), channel_id=1, replica_groups=mesh['gy_0'=2,'gy_1'=4,'gy_2'=2,'gx_0'=2,'gx_1'=8] {'gx_0'}, use_global_device_ids=true, to_apply=%region_5.6 | all-reduce | flops 2 | bytes 16 | tf_op jit(solution)/shard_map/psum | solution.py:30
  112.2 14.6 %all-reduce.2 = (f32[]{:T(128)}, f32[]{:T(128)}) all-reduce(f32[]{:T(128)} %get-tuple-element.26, f32[]{:T(128)} %get-tuple-element.27), channel_id=1, replica_groups=mesh['gy_0'=2,'gy_1'=4,'gy_2'=2,'gx_0'=2,'gx_1'=8] {'gx_1'}, use_global_device_ids=true, to_apply=%region_6.7 | all-reduce | flops 2 | bytes 16 | tf_op jit(solution)/shard_map/psum | solution.py:30
  128.2 6.4 %collective-permute-start.16 = (f32[1,256]{1,0:T(1,128)S(1)}, f32[1,256]{1,0:T(1,128)S(1)}, u32[]{:S(2)}, u32[]{:S(2)}) collective-permute-start(f32[1,256]{1,0:T(1,128)S(1)} %get-tuple-element.70), channel_id=1, source_target_pairs={{0,16},{16,32},{32,48},{48,64},{64,80},{80,96},{96,112},{112,128},... | collective-permute-start | bytes 3080 | tf_op jit(solution)/shard_map/ppermute | solution.py:23
  135.3 2.6 %collective-permute-done.17 = f32[1,256]{1,0:T(1,128)S(1)} collective-permute-done((f32[1,256]{1,0:T(1,128)S(1)}, f32[1,256]{1,0:T(1,128)S(1)}, u32[]{:S(2)}, u32[]{:S(2)}) %collective-permute-start.17) | collective-permute-done | bytes 1056 | tf_op jit(solution)/shard_map/ppermute | solution.py:24
  138.0 5.1 %collective-permute-start.19 = (f32[130,1]{1,0:T(8,128)S(1)}, f32[130,1]{1,0:T(8,128)S(1)}, u32[]{:S(2)}, u32[]{:S(2)}) collective-permute-start(f32[130,1]{1,0:T(8,128)S(1)} %get-tuple-element.65), channel_id=1, source_target_pairs={{1,0},{2,1},{3,2},{4,3},{5,4},{6,5},{7,6},{8,7},{9,8},{10,9},{11,1... | collective-permute-start | bytes 1568 | tf_op jit(solution)/shard_map/ppermute | solution.py:24
  143.1 1.7 collective-permute-done.18
  145.9 4.4 %all-reduce.13 = (f32[]{:T(128)}, f32[]{:T(128)}) all-reduce(f32[]{:T(128)} %get-tuple-element.7, f32[]{:T(128)} %get-tuple-element.6), channel_id=1, replica_groups=mesh['gy_0'=2,'gy_1'=4,'gy_2'=2,'gx_0'=2,'gx_1'=8] {'gy_0'}, use_global_device_ids=true, to_apply=%region_14.15 | all-reduce | flops 2 | bytes 16 | tf_op jit(solution)/shard_map/psum | solution.py:30
  150.3 10.5 %all-reduce.4 = (f32[]{:T(128)}, f32[]{:T(128)}) all-reduce(f32[]{:T(128)} %get-tuple-element.36, f32[]{:T(128)} %get-tuple-element.37), channel_id=1, replica_groups=mesh['gy_0'=2,'gy_1'=4,'gy_2'=2,'gx_0'=2,'gx_1'=8] {'gy_1'}, use_global_device_ids=true, to_apply=%region_15.16 | all-reduce | flops 2 | bytes 16 | tf_op jit(solution)/shard_map/psum | solution.py:30
  160.7 3.8 %all-reduce.10 = (f32[]{:T(128)}, f32[]{:T(128)}) all-reduce(f32[]{:T(128)} %get-tuple-element.18, f32[]{:T(128)} %get-tuple-element.19), channel_id=1, replica_groups=mesh['gy_0'=2,'gy_1'=4,'gy_2'=2,'gx_0'=2,'gx_1'=8] {'gy_2'}, use_global_device_ids=true, to_apply=%region_16.17 | all-reduce | flops 2 | bytes 16 | tf_op jit(solution)/shard_map/psum | solution.py:30
  164.5 6.0 %all-reduce.7 = (f32[]{:T(128)}, f32[]{:T(128)}) all-reduce(f32[]{:T(128)} %get-tuple-element.30, f32[]{:T(128)} %get-tuple-element.31), channel_id=1, replica_groups=mesh['gy_0'=2,'gy_1'=4,'gy_2'=2,'gx_0'=2,'gx_1'=8] {'gx_0'}, use_global_device_ids=true, to_apply=%region_17.18 | all-reduce | flops 2 | bytes 16 | tf_op jit(solution)/shard_map/psum | solution.py:30
  170.5 16.4 %all-reduce.1 = (f32[]{:T(128)}, f32[]{:T(128)}) all-reduce(f32[]{:T(128)} %get-tuple-element.24, f32[]{:T(128)} %get-tuple-element.25), channel_id=1, replica_groups=mesh['gy_0'=2,'gy_1'=4,'gy_2'=2,'gx_0'=2,'gx_1'=8] {'gx_1'}, use_global_device_ids=true, to_apply=%region_18.19 | all-reduce | flops 2 | bytes 16 | tf_op jit(solution)/shard_map/psum | solution.py:30
  191.4 6.9 %collective-permute-start.20 = (f32[1,256]{1,0:T(1,128)S(1)}, f32[1,256]{1,0:T(1,128)S(1)}, u32[]{:S(2)}, u32[]{:S(2)}) collective-permute-start(f32[1,256]{1,0:T(1,128)S(1)} %get-tuple-element.68), channel_id=1, source_target_pairs={{0,16},{16,32},{32,48},{48,64},{64,80},{80,96},{96,112},{112,128},... | collective-permute-start | bytes 3080 | tf_op jit(solution)/shard_map/ppermute | solution.py:23
  199.0 2.4 collective-permute-done.21
  201.6 5.1 %collective-permute-start.23 = (f32[130,1]{1,0:T(8,128)S(1)}, f32[130,1]{1,0:T(8,128)S(1)}, u32[]{:S(2)}, u32[]{:S(2)}) collective-permute-start(f32[130,1]{1,0:T(8,128)S(1)} %get-tuple-element.63), channel_id=1, source_target_pairs={{1,0},{2,1},{3,2},{4,3},{5,4},{6,5},{7,6},{8,7},{9,8},{10,9},{11,1... | collective-permute-start | bytes 1568 | tf_op jit(solution)/shard_map/ppermute | solution.py:24
  206.6 1.7 collective-permute-done.22
  209.4 4.4 %all-reduce.12 = (f32[]{:T(128)}, f32[]{:T(128)}) all-reduce(f32[]{:T(128)} %get-tuple-element.5, f32[]{:T(128)} %get-tuple-element.4), channel_id=1, replica_groups=mesh['gy_0'=2,'gy_1'=4,'gy_2'=2,'gx_0'=2,'gx_1'=8] {'gy_0'}, use_global_device_ids=true, to_apply=%region_26.27 | all-reduce | flops 2 | bytes 16 | tf_op jit(solution)/shard_map/psum | solution.py:30
  213.8 9.8 %all-reduce.3 = (f32[]{:T(128)}, f32[]{:T(128)}) all-reduce(f32[]{:T(128)} %get-tuple-element.34, f32[]{:T(128)} %get-tuple-element.35), channel_id=1, replica_groups=mesh['gy_0'=2,'gy_1'=4,'gy_2'=2,'gx_0'=2,'gx_1'=8] {'gy_1'}, use_global_device_ids=true, to_apply=%region_27.28 | all-reduce | flops 2 | bytes 16 | tf_op jit(solution)/shard_map/psum | solution.py:30
  223.6 4.0 %all-reduce.9 = (f32[]{:T(128)}, f32[]{:T(128)}) all-reduce(f32[]{:T(128)} %get-tuple-element.16, f32[]{:T(128)} %get-tuple-element.17), channel_id=1, replica_groups=mesh['gy_0'=2,'gy_1'=4,'gy_2'=2,'gx_0'=2,'gx_1'=8] {'gy_2'}, use_global_device_ids=true, to_apply=%region_28.29 | all-reduce | flops 2 | bytes 16 | tf_op jit(solution)/shard_map/psum | solution.py:30
  227.6 5.9 %all-reduce.6 = (f32[]{:T(128)}, f32[]{:T(128)}) all-reduce(f32[]{:T(128)} %get-tuple-element.28, f32[]{:T(128)} %get-tuple-element.29), channel_id=1, replica_groups=mesh['gy_0'=2,'gy_1'=4,'gy_2'=2,'gx_0'=2,'gx_1'=8] {'gx_0'}, use_global_device_ids=true, to_apply=%region_29.30 | all-reduce | flops 2 | bytes 16 | tf_op jit(solution)/shard_map/psum | solution.py:30
  233.5 14.6 %all-reduce = (f32[]{:T(128)}, f32[]{:T(128)}) all-reduce(f32[]{:T(128)} %get-tuple-element.22, f32[]{:T(128)} %get-tuple-element.23), channel_id=1, replica_groups=mesh['gy_0'=2,'gy_1'=4,'gy_2'=2,'gx_0'=2,'gx_1'=8] {'gx_1'}, use_global_device_ids=true, to_apply=%region_30.31 | all-reduce | flops 2 | bytes 16 | tf_op jit(solution)/shard_map/psum | solution.py:30
  (89 shorter events, 17.4 us)
Async XLA Ops:
  0.6 5.4 %copy-start.3 = (f32[8,128,256]{2,1,0:T(8,128)S(1)}, f32[8,128,256]{2,1,0:T(8,128)}, u32[]{:S(2)}) copy-start(f32[8,128,256]{2,1,0:T(8,128)} %param.9) | copy-start | bytes 3145732
  1.6 9.3 %collective-permute-start.4 = (f32[8,1,256]{2,1,0:T(1,128)S(1)}, f32[8,1,256]{2,1,0:T(1,128)S(1)}, u32[]{:S(2)}, u32[]{:S(2)}) collective-permute-start(f32[8,1,256]{2,1,0:T(1,128)S(1)} %get-tuple-element.61), channel_id=1, source_target_pairs={{0,16},{16,32},{32,48},{48,64},{64,80},{80,96},{96,112},{112,128},... | collective-permute-start | bytes 24584 | tf_op jit(solution)/shard_map/ppermute | solution.py:23
  4.3 6.7 %collective-permute-start.5 = (f32[8,1,256]{2,1,0:T(1,128)S(1)}, f32[8,1,256]{2,1,0:T(1,128)S(1)}, u32[]{:S(2)}, u32[]{:S(2)}) collective-permute-start(f32[8,1,256]{2,1,0:T(1,128)S(1)} %get-tuple-element.60), channel_id=1, source_target_pairs={{16,0},{32,16},{48,32},{64,48},{80,64},{96,80},{112,96},{128,112},... | collective-permute-start | bytes 24584 | tf_op jit(solution)/shard_map/ppermute | solution.py:24
  6.0 5.0 %copy-start = (f32[8,128,256]{2,1,0:T(8,128)S(1)}, f32[8,128,256]{2,1,0:T(8,128)}, u32[]{:S(2)}) copy-start(f32[8,128,256]{2,1,0:T(8,128)} %param.7) | copy-start | bytes 3145732
  7.0 11.5 %collective-permute-start = (f32[3,8,1,256]{3,2,1,0:T(1,128)S(1)}, f32[3,8,1,256]{3,2,1,0:T(1,128)S(1)}, u32[]{:S(2)}, u32[]{:S(2)}) collective-permute-start(f32[3,8,1,256]{3,2,1,0:T(1,128)S(1)} %get-tuple-element.52), channel_id=1, source_target_pairs={{0,16},{16,32},{32,48},{48,64},{64,80},{80,96},{96,112},{112,128},... | collective-permute-start | bytes 73736 | tf_op jit(solution)/shard_map/ppermute | solution.py:23
  8.1 10.4 %collective-permute-start.1 = (f32[3,8,1,256]{3,2,1,0:T(1,128)S(1)}, f32[3,8,1,256]{3,2,1,0:T(1,128)S(1)}, u32[]{:S(2)}, u32[]{:S(2)}) collective-permute-start(f32[3,8,1,256]{3,2,1,0:T(1,128)S(1)} %get-tuple-element.53), channel_id=1, source_target_pairs={{16,0},{32,16},{48,32},{64,48},{80,64},{96,80},{112,96},{128,112},... | collective-permute-start | bytes 73736 | tf_op jit(solution)/shard_map/ppermute | solution.py:24
  11.6 21.1 %collective-permute-start.6 = (f32[8,130,1]{1,0,2:T(8,128)S(1)}, f32[8,130,1]{1,0,2:T(8,128)S(1)}, u32[]{:S(2)}, u32[]{:S(2)}) collective-permute-start(f32[8,130,1]{1,0,2:T(8,128)S(1)} %copy.27), channel_id=1, source_target_pairs={{0,1},{1,2},{2,3},{3,4},{4,5},{5,6},{6,7},{7,8},{8,9},{9,10},{10,1... | collective-permute-start | bytes 12488 | tf_op jit(solution)/shard_map/ppermute | solution.py:23
  12.0 20.9 %collective-permute-start.7 = (f32[8,130,1]{1,0,2:T(8,128)S(1)}, f32[8,130,1]{1,0,2:T(8,128)S(1)}, u32[]{:S(2)}, u32[]{:S(2)}) collective-permute-start(f32[8,130,1]{1,0,2:T(8,128)S(1)} %copy.29), channel_id=1, source_target_pairs={{1,0},{2,1},{3,2},{4,3},{5,4},{6,5},{7,6},{8,7},{9,8},{10,9},{11,1... | collective-permute-start | bytes 12488 | tf_op jit(solution)/shard_map/ppermute | solution.py:24
  25.0 9.0 %collective-permute-start.2 = (f32[3,8,130,1]{2,1,3,0:T(8,128)S(1)}, f32[3,8,130,1]{2,1,3,0:T(8,128)S(1)}, u32[]{:S(2)}, u32[]{:S(2)}) collective-permute-start(f32[3,8,130,1]{2,1,3,0:T(8,128)S(1)} %copy.23), channel_id=1, source_target_pairs={{0,1},{1,2},{2,3},{3,4},{4,5},{5,6},{6,7},{7,8},{8,9},{9,10},{10,1... | collective-permute-start | bytes 37448 | tf_op jit(solution)/shard_map/ppermute | solution.py:23
  27.4 8.4 %collective-permute-start.3 = (f32[3,8,130,1]{2,1,3,0:T(8,128)S(1)}, f32[3,8,130,1]{2,1,3,0:T(8,128)S(1)}, u32[]{:S(2)}, u32[]{:S(2)}) collective-permute-start(f32[3,8,130,1]{2,1,3,0:T(8,128)S(1)} %copy.24), channel_id=1, source_target_pairs={{1,0},{2,1},{3,2},{4,3},{5,4},{6,5},{7,6},{8,7},{9,8},{10,9},{11,1... | collective-permute-start | bytes 37448 | tf_op jit(solution)/shard_map/ppermute | solution.py:24
  43.5 1.2 copy-start.5
  43.5 2.2 copy-start.2
  44.6 1.1 copy-start.7
  45.7 1.3 copy-start.1
  47.4 5.4 %collective-permute-start.8 = (f32[8,1,256]{2,1,0:T(1,128)S(1)}, f32[8,1,256]{2,1,0:T(1,128)S(1)}, u32[]{:S(2)}, u32[]{:S(2)}) collective-permute-start(f32[8,1,256]{2,1,0:T(1,128)S(1)} %get-tuple-element.59), channel_id=1, source_target_pairs={{0,16},{16,32},{32,48},{48,64},{64,80},{80,96},{96,112},{112,128},... | collective-permute-start | bytes 24584 | tf_op jit(solution)/shard_map/ppermute | solution.py:23
  48.9 4.0 %collective-permute-start.9 = (f32[8,1,256]{2,1,0:T(1,128)S(1)}, f32[8,1,256]{2,1,0:T(1,128)S(1)}, u32[]{:S(2)}, u32[]{:S(2)}) collective-permute-start(f32[8,1,256]{2,1,0:T(1,128)S(1)} %get-tuple-element.58), channel_id=1, source_target_pairs={{16,0},{32,16},{48,32},{64,48},{80,64},{96,80},{112,96},{128,112},... | collective-permute-start | bytes 24584 | tf_op jit(solution)/shard_map/ppermute | solution.py:24
  55.5 9.1 %collective-permute-start.10 = (f32[8,130,1]{1,0,2:T(8,128)S(1)}, f32[8,130,1]{1,0,2:T(8,128)S(1)}, u32[]{:S(2)}, u32[]{:S(2)}) collective-permute-start(f32[8,130,1]{1,0,2:T(8,128)S(1)} %copy.31), channel_id=1, source_target_pairs={{0,1},{1,2},{2,3},{3,4},{4,5},{5,6},{6,7},{7,8},{8,9},{9,10},{10,1... | collective-permute-start | bytes 12488 | tf_op jit(solution)/shard_map/ppermute | solution.py:23
  55.9 9.0 %collective-permute-start.11 = (f32[8,130,1]{1,0,2:T(8,128)S(1)}, f32[8,130,1]{1,0,2:T(8,128)S(1)}, u32[]{:S(2)}, u32[]{:S(2)}) collective-permute-start(f32[8,130,1]{1,0,2:T(8,128)S(1)} %copy.33), channel_id=1, source_target_pairs={{1,0},{2,1},{3,2},{4,3},{5,4},{6,5},{7,6},{8,7},{9,8},{10,9},{11,1... | collective-permute-start | bytes 12488 | tf_op jit(solution)/shard_map/ppermute | solution.py:24
  65.9 2.8 %copy-start.4 = (f32[8,129,256]{2,1,0:T(8,128)S(1)}, f32[8,129,256]{2,1,0:T(8,128)}, u32[]{:S(2)}) copy-start(f32[8,129,256]{2,1,0:T(8,128)} %fusion.12) | copy-start | bytes 3170308
  65.9 2.8 %copy-start.8 = (s32[128,256]{1,0:T(8,128)S(1)}, s32[128,256]{1,0:T(8,128)}, u32[]{:S(2)}) copy-start(s32[128,256]{1,0:T(8,128)} %param.10) | copy-start | bytes 393220
  65.9 2.8 %copy-start.10 = (f32[8]{0:T(128)S(1)}, f32[8]{0:T(128)}, u32[]{:S(2)}) copy-start(f32[8]{0:T(128)} %param.11) | copy-start | bytes 100
  68.8 1.5 copy-start.6
  68.8 1.5 copy-start.9
  70.4 5.6 %collective-permute-start.12 = (f32[1,256]{1,0:T(1,128)S(1)}, f32[1,256]{1,0:T(1,128)S(1)}, u32[]{:S(2)}, u32[]{:S(2)}) collective-permute-start(f32[1,256]{1,0:T(1,128)S(1)} %get-tuple-element.72), channel_id=1, source_target_pairs={{0,16},{16,32},{32,48},{48,64},{64,80},{80,96},{96,112},{112,128},... | collective-permute-start | bytes 3080 | tf_op jit(solution)/shard_map/ppermute | solution.py:23
  70.4 5.8 %collective-permute-start.13 = (f32[1,256]{1,0:T(1,128)S(1)}, f32[1,256]{1,0:T(1,128)S(1)}, u32[]{:S(2)}, u32[]{:S(2)}) collective-permute-start(f32[1,256]{1,0:T(1,128)S(1)} %get-tuple-element.73), channel_id=1, source_target_pairs={{16,0},{32,16},{48,32},{64,48},{80,64},{96,80},{112,96},{128,112},... | collective-permute-start | bytes 3080 | tf_op jit(solution)/shard_map/ppermute | solution.py:24
  76.3 6.8 %collective-permute-start.14 = (f32[130,1]{1,0:T(8,128)S(1)}, f32[130,1]{1,0:T(8,128)S(1)}, u32[]{:S(2)}, u32[]{:S(2)}) collective-permute-start(f32[130,1]{1,0:T(8,128)S(1)} %get-tuple-element.66), channel_id=1, source_target_pairs={{0,1},{1,2},{2,3},{3,4},{4,5},{5,6},{6,7},{7,8},{8,9},{9,10},{10,1... | collective-permute-start | bytes 1568 | tf_op jit(solution)/shard_map/ppermute | solution.py:23
  76.4 6.8 %collective-permute-start.15 = (f32[130,1]{1,0:T(8,128)S(1)}, f32[130,1]{1,0:T(8,128)S(1)}, u32[]{:S(2)}, u32[]{:S(2)}) collective-permute-start(f32[130,1]{1,0:T(8,128)S(1)} %get-tuple-element.67), channel_id=1, source_target_pairs={{1,0},{2,1},{3,2},{4,3},{5,4},{6,5},{7,6},{8,7},{9,8},{10,9},{11,1... | collective-permute-start | bytes 1568 | tf_op jit(solution)/shard_map/ppermute | solution.py:24
  128.2 7.1 %collective-permute-start.16 = (f32[1,256]{1,0:T(1,128)S(1)}, f32[1,256]{1,0:T(1,128)S(1)}, u32[]{:S(2)}, u32[]{:S(2)}) collective-permute-start(f32[1,256]{1,0:T(1,128)S(1)} %get-tuple-element.70), channel_id=1, source_target_pairs={{0,16},{16,32},{32,48},{48,64},{64,80},{80,96},{96,112},{112,128},... | collective-permute-start | bytes 3080 | tf_op jit(solution)/shard_map/ppermute | solution.py:23
  134.5 3.3 %collective-permute-start.17 = (f32[1,256]{1,0:T(1,128)S(1)}, f32[1,256]{1,0:T(1,128)S(1)}, u32[]{:S(2)}, u32[]{:S(2)}) collective-permute-start(f32[1,256]{1,0:T(1,128)S(1)} %get-tuple-element.71), channel_id=1, source_target_pairs={{16,0},{32,16},{48,32},{64,48},{80,64},{96,80},{112,96},{128,112},... | collective-permute-start | bytes 3080 | tf_op jit(solution)/shard_map/ppermute | solution.py:24
  137.9 6.8 %collective-permute-start.18 = (f32[130,1]{1,0:T(8,128)S(1)}, f32[130,1]{1,0:T(8,128)S(1)}, u32[]{:S(2)}, u32[]{:S(2)}) collective-permute-start(f32[130,1]{1,0:T(8,128)S(1)} %get-tuple-element.64), channel_id=1, source_target_pairs={{0,1},{1,2},{2,3},{3,4},{4,5},{5,6},{6,7},{7,8},{8,9},{9,10},{10,1... | collective-permute-start | bytes 1568 | tf_op jit(solution)/shard_map/ppermute | solution.py:23
  138.0 6.8 %collective-permute-start.19 = (f32[130,1]{1,0:T(8,128)S(1)}, f32[130,1]{1,0:T(8,128)S(1)}, u32[]{:S(2)}, u32[]{:S(2)}) collective-permute-start(f32[130,1]{1,0:T(8,128)S(1)} %get-tuple-element.65), channel_id=1, source_target_pairs={{1,0},{2,1},{3,2},{4,3},{5,4},{6,5},{7,6},{8,7},{9,8},{10,9},{11,1... | collective-permute-start | bytes 1568 | tf_op jit(solution)/shard_map/ppermute | solution.py:24
  191.4 7.6 %collective-permute-start.20 = (f32[1,256]{1,0:T(1,128)S(1)}, f32[1,256]{1,0:T(1,128)S(1)}, u32[]{:S(2)}, u32[]{:S(2)}) collective-permute-start(f32[1,256]{1,0:T(1,128)S(1)} %get-tuple-element.68), channel_id=1, source_target_pairs={{0,16},{16,32},{32,48},{48,64},{64,80},{80,96},{96,112},{112,128},... | collective-permute-start | bytes 3080 | tf_op jit(solution)/shard_map/ppermute | solution.py:23
  198.3 3.1 %collective-permute-start.21 = (f32[1,256]{1,0:T(1,128)S(1)}, f32[1,256]{1,0:T(1,128)S(1)}, u32[]{:S(2)}, u32[]{:S(2)}) collective-permute-start(f32[1,256]{1,0:T(1,128)S(1)} %get-tuple-element.69), channel_id=1, source_target_pairs={{16,0},{32,16},{48,32},{64,48},{80,64},{96,80},{112,96},{128,112},... | collective-permute-start | bytes 3080 | tf_op jit(solution)/shard_map/ppermute | solution.py:24
  201.5 6.8 %collective-permute-start.22 = (f32[130,1]{1,0:T(8,128)S(1)}, f32[130,1]{1,0:T(8,128)S(1)}, u32[]{:S(2)}, u32[]{:S(2)}) collective-permute-start(f32[130,1]{1,0:T(8,128)S(1)} %get-tuple-element.62), channel_id=1, source_target_pairs={{0,1},{1,2},{2,3},{3,4},{4,5},{5,6},{6,7},{7,8},{8,9},{9,10},{10,1... | collective-permute-start | bytes 1568 | tf_op jit(solution)/shard_map/ppermute | solution.py:23
  201.6 6.8 %collective-permute-start.23 = (f32[130,1]{1,0:T(8,128)S(1)}, f32[130,1]{1,0:T(8,128)S(1)}, u32[]{:S(2)}, u32[]{:S(2)}) collective-permute-start(f32[130,1]{1,0:T(8,128)S(1)} %get-tuple-element.63), channel_id=1, source_target_pairs={{1,0},{2,1},{3,2},{4,3},{5,4},{6,5},{7,6},{8,7},{9,8},{10,9},{11,1... | collective-permute-start | bytes 1568 | tf_op jit(solution)/shard_map/ppermute | solution.py:24
where the time goes:
time: 258 us; the launch traced here: 253 us
  blocking collectives  122 us (47%)
  starting transfers between devices  63.1 us (24%)
  other arithmetic  24.3 us (9%)
  local copies, waits for them, and re-layouts  19.2 us (7%)
  waiting for transfers between devices  13.1 us (5%)
  between operations  10.5 us (4%)
    psum x15, blocking collectives, over_axes(): return functools.reduce(lax.psum, axes, array)  122 us
    ppermute x12, starting transfers between devices, extended_2(): after = lax.ppermute(first, axis, down)  44 us
    ppermute x12, starting transfers between devices, extended_2(): before = lax.ppermute(last, axis, up)  19.1 us
    concatenate x7, other arithmetic, extended_2(): array = jnp.concatenate([before, array, after], axis=dim)  7.82 us
    slice x12, local copies, waits for them, and re-layouts, extended_2(): last = lax.slice_in_dim(array, length - width, length, axis=dim)  7.76 us
    ppermute x12, waiting for transfers between devices, extended_2(): before = lax.ppermute(last, axis, up)  7.66 us
    ppermute x12, waiting for transfers between devices, extended_2(): after = lax.ppermute(first, axis, down)  5.47 us
  transfers between devices with their start and end apart: 24, of which 11 were waited for; matrix products, arithmetic and copies ran while one was open for 7% of the time, Pallas kernels for 0%

commit v1 on v0

v1 whole, which is shorter than its diff:
```python
import functools

import jax
import jax.numpy as jnp
from jax import lax
from jax.experimental import pallas as pl
from jax.experimental.pallas import tpu as pltpu
from jax.sharding import PartitionSpec as P

TSTEPS = 2
ITERS = 3
K = 8
R, C = 128, 256
RE, CE = R + 16, C + 128
HALO = 5
MESH = pl.DeviceIdType.MESH
TR, EA, NO, SF, HE, CO = 0, K, 2 * K, 3 * K, 3 * K + 1, 3 * K + 2
NF = 3 * K + 2


def lane_plan():
    first, last = [], []
    for plan, widths in ((first, (5, 4, 4)), (last, (5, 5, 4))):
        lane = 0
        for base, width in zip((TR, EA, NO), widths):
            for k in range(K):
                plan.append((base + k, width, lane))
                lane += width
        for field, width in ((SF, 3), (HE, 3), (CO, 5)):
            plan.append((field, width, lane))
            lane += width
        assert lane <= 128
    return first, last


FIRST, LAST = lane_plan()


def up(now, nxt, sub):
    return pltpu.roll(jnp.where(sub == 0, nxt, now), 7, 0)


def down(now, prv, sub):
    return pltpu.roll(jnp.where(sub == 7, prv, now), 1, 0)


def east(a):
    return pltpu.roll(a, CE - 1, 1)


def west(a):
    return pltpu.roll(a, 1, 1)


def kernel(
    ngy, ngx,
    tr_hbm, ea_hbm, no_hbm, co_hbm, th, sf_hbm, he_hbm,
    tr_out, h_out,
    a, ci, c1, pw, pe, re, rw, me_s, mn_s, f_s, inv_s, v1_s, v2_s, row, b1, b2,
    load_sem, send_sem, recv_sem, rs_sem, rr_sem,
):
    gy, gx = lax.axis_index("gy"), lax.axis_index("gx")
    north, south = lax.rem(gy + 1, ngy), lax.rem(gy + ngy - 1, ngy)
    e_id, w_id = lax.rem(gx + 1, ngx), lax.rem(gx + ngx - 1, ngx)
    hi, z = lax.div(gx, 8), lax.rem(gx, 8)
    group1 = [
        (lax.rem(gy + dy, ngy), lax.rem(gx + 8 * dh, ngx))
        for dh in range(2) for dy in range(16) if dy or dh
    ]
    group2 = [(gy, hi * 8 + lax.rem(z + dz, 8)) for dz in range(1, 8)]
    near = [(north, gx), (south, gx), (gy, e_id), (gy, w_id),
            (north, e_id), (north, w_id), (south, e_id), (south, w_id)]

    barrier = pltpu.get_barrier_semaphore()
    for y, x in near + group1 + group2:
        pl.semaphore_signal(barrier, inc=1, device_id={"gy": y, "gx": x}, device_id_type=MESH)

    own = (pl.ds(8, R), pl.ds(0, C))
    loads = [
        pltpu.make_async_copy(src, dst, load_sem.at[i])
        for i, (src, dst) in enumerate((
            (tr_hbm, a.at[(pl.ds(TR, K),) + own]),
            (ea_hbm, a.at[(pl.ds(EA, K),) + own]),
            (no_hbm, a.at[(pl.ds(NO, K),) + own]),
            (sf_hbm, a.at[(SF,) + own]),
            (he_hbm, a.at[(HE,) + own]),
            (co_hbm, ci.at[own]),
        ))
    ]
    for copy in loads:
        copy.start()
    for copy in loads:
        copy.wait()

    lane = lax.broadcasted_iota(jnp.int32, (R, 128), 1)

    def edge(field, side):
        cols = pl.ds(0 if side == 0 else C - 128, 128)
        if field == CO:
            return ci[pl.ds(8, R), cols].astype(jnp.float32)
        return a[field, pl.ds(8, R), cols]

    for side, plan, dest in ((0, FIRST, pw), (1, LAST, pe)):
        tile = jnp.zeros((R, 128), jnp.float32)
        for field, width, at in plan:
            start = 0 if side == 0 else 128 - width
            value = edge(field, side)
            shift = (at - start) % 128
            if shift:
                value = pltpu.roll(value, shift, 1)
            tile = jnp.where((lane >= at) & (lane < at + width), value, tile)
        dest[...] = tile

    pl.semaphore_wait(barrier, len(near) + len(group1) + len(group2))

    top, bottom = pl.ds(R, 8), pl.ds(8, 8)
    ghost_s, ghost_n = pl.ds(0, 8), pl.ds(R + 8, 8)
    cols = pl.ds(0, C)
    every = pl.ds(0, NF)
    routes = [
        (pe, rw.at[pl.ds(8, R)], (gy, e_id)),
        (pw, re.at[pl.ds(8, R)], (gy, w_id)),
        (a.at[every, top, cols], a.at[every, ghost_s, cols], (north, gx)),
        (a.at[every, bottom, cols], a.at[every, ghost_n, cols], (south, gx)),
        (ci.at[top, cols], ci.at[ghost_s, cols], (north, gx)),
        (ci.at[bottom, cols], ci.at[ghost_n, cols], (south, gx)),
        (pe.at[pl.ds(R - 8, 8)], rw.at[ghost_s], (north, e_id)),
        (pw.at[pl.ds(R - 8, 8)], re.at[ghost_s], (north, w_id)),
        (pe.at[pl.ds(0, 8)], rw.at[ghost_n], (south, e_id)),
        (pw.at[pl.ds(0, 8)], re.at[ghost_n], (south, w_id)),
    ]
    sends = [
        pltpu.make_async_remote_copy(
            src_ref=src, dst_ref=dst, send_sem=send_sem.at[i], recv_sem=recv_sem.at[i],
            device_id={"gy": y, "gx": x}, device_id_type=MESH,
        )
        for i, (src, dst, (y, x)) in enumerate(routes)
    ]
    for copy in sends:
        copy.start()
    for copy in sends:
        copy.wait_recv()

    lane_e = lax.broadcasted_iota(jnp.int32, (RE, 128), 1)
    last_at = {field: (width, at) for field, width, at in LAST}
    ghost = pl.ds(C, 128)
    for field, width, at in FIRST:
        from_east = re[...]
        if at:
            from_east = pltpu.roll(from_east, 128 - at, 1)
        wide, at_w = last_at[field]
        shift = (128 - wide - at_w) % 128
        from_west = rw[...]
        if shift:
            from_west = pltpu.roll(from_west, shift, 1)
        value = jnp.where(lane_e < 64, from_east, from_west)
        a[field, :, ghost] = value
    a[CO, :, cols] = ci[:, cols].astype(jnp.float32)
    zero8 = jnp.zeros((8, CE), jnp.float32)

    @pl.when(gy == 0)
    def _():
        a[CO, ghost_s, :] = zero8

    @pl.when(gy == ngy - 1)
    def _():
        a[CO, ghost_n, :] = zero8

    sub = lax.broadcasted_iota(jnp.int32, (8, CE), 0)
    tiles = RE // 8

    def rows(t):
        return pl.ds(8 * t, 8)

    for t in range(tiles):
        depth = a[CO, rows(t), :]
        above = a[CO, rows(min(t + 1, tiles - 1)), :]
        me_s[rows(t), :] = jnp.minimum(depth, east(depth))
        mn_s[rows(t), :] = jnp.minimum(depth, up(depth, above, sub))
        f_s[rows(t), :] = a[SF, rows(t), :]
        inv_s[rows(t), :] = 1.0 / (6.0 + a[HE, rows(t), :])

    def level(k, carry):
        kf = k.astype(jnp.float32)
        weight = th[k]

        def step(load, store):
            now = load(0)
            south_flux = jnp.zeros((8, CE), jnp.float32)
            for t in range(tiles):
                nxt = load(t + 1) if t + 1 < tiles else now
                es = jnp.where(me_s[rows(t), :] > kf, a[EA + k, rows(t), :], 0.0)
                ns = jnp.where(mn_s[rows(t), :] > kf, a[NO + k, rows(t), :], 0.0)
                fe = es * jnp.where(es > 0.0, now, east(now))
                fn = ns * jnp.where(ns > 0.0, now, up(now, nxt, sub))
                store(t, now - (fe - west(fe) + fn - down(fn, south_flux, sub)))
                now, south_flux = nxt, fn

        def put1(t, value):
            c1[rows(t), :] = value

        def put2(t, value):
            if 0 < t < tiles - 1:
                tr_out[k, pl.ds(8 * t - 8, 8), :] = value[:, :C]
            f_s[rows(t), :] += jnp.where(a[CO, rows(t), :] > kf, weight * value, 0.0)

        step(lambda t: a[TR + k, rows(t), :], put1)
        step(lambda t: c1[rows(t), :], put2)
        return carry

    lax.fori_loop(0, K, level, 0)

    nu = [jnp.zeros((8, C), jnp.float32) for _ in range(6)]
    for t in range(tiles):
        forcing = f_s[rows(t), :]
        z0 = forcing * inv_s[rows(t), :]
        if 0 < t < tiles - 1:
            nu[0] += (forcing * z0)[:, :C]
        c1[rows(t), :] = z0
        mn_s[rows(t), :] = jnp.where(a[CO, rows(t), :] > 0.0, 1.0, 0.0)

    def operator(src, store):
        def part(t):
            wet = mn_s[rows(t), :]
            w = wet * src[rows(t), :]
            h = west(w) + east(w)
            return wet, h, w + 0.5 * h

        wet, h, s = part(0)
        before = jnp.zeros_like(s)
        for t in range(tiles):
            after = part(t + 1) if t + 1 < tiles else (wet, h, s)
            store(t, wet * (h + up(s, after[2], sub) + down(s, before, sub)))
            before = s
            wet, h, s = after

    def store1(t, u):
        v = u * inv_s[rows(t), :]
        v1_s[rows(t), :] = v
        if 0 < t < tiles - 1:
            nu[1] += (v * f_s[rows(t), :])[:, :C]
            nu[2] += (v * u)[:, :C]

    def store2(t, u):
        v = u * inv_s[rows(t), :]
        v2_s[rows(t), :] = v
        if 0 < t < tiles - 1:
            nu[3] += (v1_s[rows(t), :] * u)[:, :C]
            nu[4] += (v * u)[:, :C]

    def store3(t, u):
        if 0 < t < tiles - 1:
            nu[5] += (v2_s[rows(t), :] * u)[:, :C]

    operator(c1, store1)
    operator(v1_s, store2)
    operator(v2_s, store3)

    lane1 = lax.broadcasted_iota(jnp.int32, (1, 128), 1)
    packed = jnp.zeros((1, 128), jnp.float32)
    for i, part in enumerate(nu):
        lanes = jnp.sum(part[:, :128] + part[:, 128:], axis=0, keepdims=True)
        total = jnp.sum(lanes, axis=1, keepdims=True)
        packed = jnp.where(lane1 == i, total, packed)

    reduce_sends = []
    for i, (group, slot, buf) in enumerate(((group1, gy * 2 + hi, b1), (group2, z, b2))):
        row[i] = packed
        n = len(group)
        for y, x in group:
            copy = pltpu.make_async_remote_copy(
                src_ref=row.at[i], dst_ref=buf.at[slot], send_sem=rs_sem.at[i], recv_sem=rr_sem.at[i],
                device_id={"gy": y, "gx": x}, device_id_type=MESH,
            )
            copy.start()
        buf[slot] = packed
        pltpu.make_async_copy(buf.at[pl.ds(0, n)], buf.at[pl.ds(0, n)], rr_sem.at[i]).wait()
        reduce_sends.append((buf, n, i))
        packed = jnp.sum(buf[...], axis=0)

    m = [jnp.sum(jnp.where(lane1 == i, packed, 0.0), axis=1, keepdims=True) for i in range(6)]

    def form(p, moments):
        total = None
        for i, pi in enumerate(p):
            for j, pj in enumerate(p[i:], i):
                term = (pi * pj if i == j else 2.0 * pi * pj) * moments[i + j]
                total = term if total is None else total + term
        return total

    diff = [m[i] - m[i + 1] for i in range(5)]
    one = jnp.ones_like(m[0])
    zc, pc = [one], [one]
    heights = [jnp.zeros_like(one)] * 3
    rz = m[0]
    for it in range(ITERS):
        alpha = rz / form(pc, diff)
        heights = [h + alpha * pc[i] if i < len(pc) else h for i, h in enumerate(heights)]
        if it + 1 < ITERS:
            applied = [p - q for p, q in zip(pc + [jnp.zeros_like(one)], [jnp.zeros_like(one)] + pc)]
            zc = [(zc[i] if i < len(zc) else 0.0) - alpha * applied[i] for i in range(len(applied))]
            rz_next = form(zc, m)
            beta = rz_next / rz
            pc = [zc[i] + beta * pc[i] if i < len(pc) else zc[i] for i in range(len(zc))]
            rz = rz_next

    inner = pl.ds(8, R)
    h_out[...] = heights[0] * c1[inner, cols] + heights[1] * v1_s[inner, cols] + heights[2] * v2_s[inner, cols]

    for copy in sends:
        copy.wait_send()
    for buf, n, i in reduce_sends:
        pltpu.make_async_copy(buf.at[pl.ds(0, n)], buf.at[pl.ds(0, n)], rs_sem.at[i]).wait()


def on_device(ngy, ngx, tracer, east_speed, north_speed, columns, thickness, surface_flux, helm):
    f32 = jnp.float32
    any_spec = pl.BlockSpec(memory_space=pltpu.HBM)
    vmem = pl.BlockSpec(memory_space=pltpu.VMEM)
    return pl.pallas_call(
        functools.partial(kernel, ngy, ngx),
        out_shape=(jax.ShapeDtypeStruct((K, R, C), f32), jax.ShapeDtypeStruct((R, C), f32)),
        in_specs=[any_spec, any_spec, any_spec, any_spec, pl.BlockSpec(memory_space=pltpu.SMEM), any_spec, any_spec],
        out_specs=(vmem, vmem),
        scratch_shapes=[
            pltpu.VMEM((NF + 1, RE, CE), f32),
            pltpu.VMEM((RE, C), jnp.int32),
            pltpu.VMEM((RE, CE), f32),
            pltpu.VMEM((R, 128), f32),
            pltpu.VMEM((R, 128), f32),
            pltpu.VMEM((RE, 128), f32),
            pltpu.VMEM((RE, 128), f32),
        ] + [pltpu.VMEM((RE, CE), f32)] * 6 + [
            pltpu.VMEM((2, 1, 128), f32),
            pltpu.VMEM((32, 1, 128), f32),
            pltpu.VMEM((8, 1, 128), f32),
            pltpu.SemaphoreType.DMA((6,)),
            pltpu.SemaphoreType.DMA((10,)),
            pltpu.SemaphoreType.DMA((10,)),
            pltpu.SemaphoreType.DMA((2,)),
            pltpu.SemaphoreType.DMA((2,)),
        ],
        compiler_params=pltpu.CompilerParams(collective_id=0, has_side_effects=True),
    )(tracer, east_speed, north_speed, columns, thickness, surface_flux, helm)


def solution(mesh):
    sizes = mesh.shape
    cells, plane = P(None, "gy", "gx"), P("gy", "gx")
    return jax.shard_map(
        functools.partial(on_device, sizes["gy"], sizes["gx"]),
        mesh=mesh,
        in_specs=(cells, cells, cells, plane, P(), plane, plane),
        out_specs=(cells, plane),
        check_vma=False,
    )
```

time: 258 us -> 35.5 us (0.14); the launches traced: 253 us -> 35.4 us
  blocking collectives: 122 us -> 0 us
  starting transfers between devices: 63.1 us -> 0 us
  Pallas kernels: 0 us -> 31.8 us
  other arithmetic: 24.3 us -> 0 us
  local copies, waits for them, and re-layouts: 19.2 us -> 2.96 us
  waiting for transfers between devices: 13.1 us -> 0 us
  between operations: 10.5 us -> 0.65 us
    psum x15 -> x0, blocking collectives: 122 us -> none  [over_axes(): return functools.reduce(lax.psum, axes, array)]
    ppermute x24 -> x0, starting transfers between devices: 63.1 us -> none  [the longest x12 44 us: extended_2(): after = lax.ppermute(first, axis, down)]
    pallas_call x0 -> x1, Pallas kernels: none -> 31.8 us  [on_device(): pl.pallas_call(functools.partial(kernel, ngy, ngx), out_shape=(jax.ShapeD...]
    ppermute x24 -> x0, waiting for transfers between devices: 13.1 us -> none  [the longest x12 7.66 us: extended_2(): before = lax.ppermute(last, axis, up)]
    slice x17 -> x0, local copies, waits for them, and re-layouts: 11.7 us -> none  [the longest x12 7.76 us: extended_2(): last = lax.slice_in_dim(array, length - width, length, axis=dim)]
    mul x8 -> x0, other arithmetic: 9.08 us -> none  [the longest x2 4.37 us: advect_block(): open_north * upwind(north_ext[:, :-1, 1:-1], extended[:, :-1, 1:-1], exte...]
    concatenate x7 -> x0, other arithmetic: 7.82 us -> none  [extended_2(): array = jnp.concatenate([before, array, after], axis=dim)]
    ppermute x6 -> x0, local copies, waits for them, and re-layouts: 6.14 us -> none  [the longest x3 3.89 us: extended_2(): after = lax.ppermute(first, axis, down)]
  transfers between devices with their start and end apart: 24 -> 0, of which waited for: 11 -> 0; matrix products, arithmetic and copies ran while one was open for 7% -> 0% of each run, Pallas kernels for 0% -> 0%
where the time goes in v1:
time: 35.5 us; the launch traced here: 35.4 us
  Pallas kernels  31.8 us (90%)
  local copies, waits for them, and re-layouts  2.96 us (8%)
  between operations  0.65 us (2%)
    pallas_call x1, Pallas kernels, on_device(): pl.pallas_call(functools.partial(kernel, ngy, ngx), out_shape=(jax.ShapeD...  31.8 us
    unnamed x4, local copies, waits for them, and re-layouts  2.96 us

profile of v1, /device:TPU:1, one launch (start us, length us, event | category | flops | bytes accessed | tf_op | source)
XLA Modules:
  0.0 35.4 jit_solution(5851279562714119662)
XLA Ops:
  0.6 31.8 %shard_map.86 = (f32[8,128,256]{2,1,0:T(8,128)}, f32[128,256]{1,0:T(8,128)}) custom-call(f32[8,128,256]{2,1,0:T(8,128)} %tr_hbm.1, f32[8,128,256]{2,1,0:T(8,128)} %ea_hbm.1, f32[8,128,256]{2,1,0:T(8,128)} %no_hbm.1, s32[128,256]{1,0:T(8,128)} %co_hbm.1, f32[8]{0:T(128)} %th.1, f32[128,256]{1,0:T(8,128)} %sf_hbm.1, f32[128,256]{1,0:T(8,128)} %he_hbm.1), custom_call_target="tpu_custom_call" | custom-call | tf_op jit(solution)/shard_map/pallas_call | solution.py:320
  32.4 0.0 copy-start
  32.4 2.3 %copy.11 = f32[8,128,256]{2,1,0:T(8,128)} copy(f32[8,128,256]{2,1,0:T(8,128)} %get-tuple-element.4) | data formatting | bytes 2097152
  34.7 0.0 copy-done
  34.7 0.7 %copy.12 = f32[128,256]{1,0:T(8,128)} copy(f32[128,256]{1,0:T(8,128)S(1)} %copy-done) | data formatting | bytes 262144
Async XLA Ops:
  32.4 2.3 %copy-start = (f32[128,256]{1,0:T(8,128)S(1)}, f32[128,256]{1,0:T(8,128)}, u32[]{:S(2)}) copy-start(f32[128,256]{1,0:T(8,128)} %get-tuple-element.5) | copy-start | bytes 393220

commit v2 on v1

--- a/solution.py
+++ b/solution.py
@@ -54,9 +54,9 @@
 
 def kernel(
     ngy, ngx,
-    tr_hbm, ea_hbm, no_hbm, co_hbm, th, sf_hbm, he_hbm,
+    tr_hbm, ea_hbm, no_hbm, co_hbm, th_hbm, sf_hbm, he_hbm,
     tr_out, h_out,
-    a, ci, c1, pw, pe, re, rw, me_s, mn_s, f_s, inv_s, v1_s, v2_s, row, b1, b2,
+    th, a, ci, c1, pw, pe, re, rw, me_s, mn_s, f_s, inv_s, v1_s, v2_s, row, b1, b2,
     load_sem, send_sem, recv_sem, rs_sem, rr_sem,
 ):
     gy, gx = lax.axis_index("gy"), lax.axis_index("gx")
@@ -85,6 +85,7 @@
             (sf_hbm, a.at[(SF,) + own]),
             (he_hbm, a.at[(HE,) + own]),
             (co_hbm, ci.at[own]),
+            (th_hbm, th),
         ))
     ]
     for copy in loads:
@@ -113,8 +114,8 @@
 
     pl.semaphore_wait(barrier, len(near) + len(group1) + len(group2))
 
-    top, bottom = pl.ds(R, 8), pl.ds(8, 8)
-    ghost_s, ghost_n = pl.ds(0, 8), pl.ds(R + 8, 8)
+    top, bottom = pl.ds(R + 3, HALO), pl.ds(8, HALO)
+    ghost_s, ghost_n = pl.ds(3, HALO), pl.ds(R + 8, HALO)
     cols = pl.ds(0, C)
     every = pl.ds(0, NF)
     routes = [
@@ -124,10 +125,10 @@
         (a.at[every, bottom, cols], a.at[every, ghost_n, cols], (south, gx)),
         (ci.at[top, cols], ci.at[ghost_s, cols], (north, gx)),
         (ci.at[bottom, cols], ci.at[ghost_n, cols], (south, gx)),
-        (pe.at[pl.ds(R - 8, 8)], rw.at[ghost_s], (north, e_id)),
-        (pw.at[pl.ds(R - 8, 8)], re.at[ghost_s], (north, w_id)),
-        (pe.at[pl.ds(0, 8)], rw.at[ghost_n], (south, e_id)),
-        (pw.at[pl.ds(0, 8)], re.at[ghost_n], (south, w_id)),
+        (pe.at[pl.ds(R - HALO, HALO)], rw.at[ghost_s], (north, e_id)),
+        (pw.at[pl.ds(R - HALO, HALO)], re.at[ghost_s], (north, w_id)),
+        (pe.at[pl.ds(0, HALO)], rw.at[ghost_n], (south, e_id)),
+        (pw.at[pl.ds(0, HALO)], re.at[ghost_n], (south, w_id)),
     ]
     sends = [
         pltpu.make_async_remote_copy(
@@ -160,11 +161,11 @@
 
     @pl.when(gy == 0)
     def _():
-        a[CO, ghost_s, :] = zero8
+        a[CO, pl.ds(0, 8), :] = zero8
 
     @pl.when(gy == ngy - 1)
     def _():
-        a[CO, ghost_n, :] = zero8
+        a[CO, pl.ds(R + 8, 8), :] = zero8
 
     sub = lax.broadcasted_iota(jnp.int32, (8, CE), 0)
     tiles = RE // 8
@@ -313,16 +314,25 @@
         pltpu.make_async_copy(buf.at[pl.ds(0, n)], buf.at[pl.ds(0, n)], rs_sem.at[i]).wait()
 
 
+def put_kernel(tr, h, tr_hbm, h_hbm, sem):
+    copies = [pltpu.make_async_copy(tr, tr_hbm, sem.at[0]), pltpu.make_async_copy(h, h_hbm, sem.at[1])]
+    for copy in copies:
+        copy.start()
+    for copy in copies:
+        copy.wait()
+
+
 def on_device(ngy, ngx, tracer, east_speed, north_speed, columns, thickness, surface_flux, helm):
     f32 = jnp.float32
     any_spec = pl.BlockSpec(memory_space=pltpu.HBM)
     vmem = pl.BlockSpec(memory_space=pltpu.VMEM)
-    return pl.pallas_call(
+    results = pl.pallas_call(
         functools.partial(kernel, ngy, ngx),
-        out_shape=(jax.ShapeDtypeStruct((K, R, C), f32), jax.ShapeDtypeStruct((R, C), f32)),
-        in_specs=[any_spec, any_spec, any_spec, any_spec, pl.BlockSpec(memory_space=pltpu.SMEM), any_spec, any_spec],
+        out_shape=(pltpu.VMEM((K, R, C), f32), pltpu.VMEM((R, C), f32)),
+        in_specs=[any_spec, any_spec, any_spec, any_spec, any_spec, any_spec, any_spec],
         out_specs=(vmem, vmem),
         scratch_shapes=[
+            pltpu.SMEM((K,), f32),
             pltpu.VMEM((NF + 1, RE, CE), f32),
             pltpu.VMEM((RE, C), jnp.int32),
             pltpu.VMEM((RE, CE), f32),
@@ -334,7 +344,7 @@
             pltpu.VMEM((2, 1, 128), f32),
             pltpu.VMEM((32, 1, 128), f32),
             pltpu.VMEM((8, 1, 128), f32),
-            pltpu.SemaphoreType.DMA((6,)),
+            pltpu.SemaphoreType.DMA((7,)),
             pltpu.SemaphoreType.DMA((10,)),
             pltpu.SemaphoreType.DMA((10,)),
             pltpu.SemaphoreType.DMA((2,)),
@@ -342,6 +352,13 @@
         ],
         compiler_params=pltpu.CompilerParams(collective_id=0, has_side_effects=True),
     )(tracer, east_speed, north_speed, columns, thickness, surface_flux, helm)
+    return pl.pallas_call(
+        put_kernel,
+        out_shape=(jax.ShapeDtypeStruct((K, R, C), f32), jax.ShapeDtypeStruct((R, C), f32)),
+        in_specs=[vmem, vmem],
+        out_specs=(any_spec, any_spec),
+        scratch_shapes=[pltpu.SemaphoreType.DMA((2,))],
+    )(*[pltpu.with_memory_space_constraint(r, pltpu.VMEM) for r in results])
 
 
 def solution(mesh):

time: 35.5 us -> 31.5 us (0.89)
  local copies, waits for them, and re-layouts: 2.96 us -> 0 us
  Pallas kernels: 31.8 us -> 30.8 us
    unnamed x4 -> x0, local copies, waits for them, and re-layouts: 2.96 us -> none
    pallas_call x1 -> x2, Pallas kernels: 31.8 us -> 30.8 us  [the longest x1 29.8 us: on_device(): pl.pallas_call(functools.partial(kernel, ngy, ngx), out_shape=(pltpu.VMEM...]
where the time goes in v2:
time: 31.5 us
  Pallas kernels  30.8 us (98%)
  between operations  0.64 us (2%)
    pallas_call x1, Pallas kernels, on_device(): pl.pallas_call(functools.partial(kernel, ngy, ngx), out_shape=(pltpu.VMEM...  29.8 us
    pallas_call x1, Pallas kernels, on_device(): pl.pallas_call(put_kernel, out_shape=(jax.ShapeDtypeStruct((K, R, C), f32...  1.02 us

profile of v2, /device:TPU:1, one launch (start us, length us, event | category | flops | bytes accessed | tf_op | source)
XLA Modules:
  0.0 31.5 jit_solution(9107113838546111226)
XLA Ops:
  0.6 29.8 %shard_map.86 = (f32[8,128,256]{2,1,0:T(8,128)S(1)}, f32[128,256]{1,0:T(8,128)S(1)}) custom-call(f32[8,128,256]{2,1,0:T(8,128)} %tr_hbm.1, f32[8,128,256]{2,1,0:T(8,128)} %ea_hbm.1, f32[8,128,256]{2,1,0:T(8,128)} %no_hbm.1, s32[128,256]{1,0:T(8,128)} %co_hbm.1, f32[8]{0:T(128)} %th_hbm.1, f32[128,256]{1,0:T(8,128)} %sf_hbm.1, f32[128,256]{1,0:T(8,128)} %he_hbm.1), custom_call_target="tpu_custom_call" | custom-call | tf_op jit(solution)/shard_map/pallas_call | solution.py:329
  30.4 1.0 %shard_map.87 = (f32[8,128,256]{2,1,0:T(8,128)}, f32[128,256]{1,0:T(8,128)}) custom-call(f32[8,128,256]{2,1,0:T(8,128)S(1)} %get-tuple-element.4.tr, f32[128,256]{1,0:T(8,128)S(1)} %get-tuple-element.5.h), custom_call_target="tpu_custom_call" | custom-call | tf_op jit(solution)/shard_map/pallas_call | solution.py:355

commit v3 on v2

v3 whole, which is shorter than its diff:
```python
import functools

import jax
import jax.numpy as jnp
from jax import lax
from jax.experimental import pallas as pl
from jax.experimental.pallas import tpu as pltpu
from jax.sharding import PartitionSpec as P

ITERS = 3
K = 8
R, C, L = 128, 256, 128
RE = R + 24
HALO = 5
MESH = pl.DeviceIdType.MESH
TR, EA, NO, SF, HE, CO = 0, K, 2 * K, 3 * K, 3 * K + 1, 3 * K + 2
NF = 3 * K + 2
UNROLL = 2


def lane_plan():
    order = []
    for k in range(K):
        order += [(TR + k, 5, 5), (EA + k, 4, 5), (NO + k, 4, 4)]
    order += [(SF, 3, 3), (HE, 3, 3), (CO, 5, 5)]
    plan, at = [], 0
    for i, (field, first, last) in enumerate(order):
        if i:
            at += max(order[i - 1][1], last)
        plan.append((field, at, first, last))
    assert at + 5 <= L - 4
    return plan


PLAN = lane_plan()


def window(lane, start, width):
    start %= L
    if start + width <= L:
        return (lane >= start) & (lane < start + width)
    return (lane >= start) | (lane < start + width - L)


def turn(a, shift):
    shift %= L
    return pltpu.roll(a, shift, 1) if shift else a


def ring_east(tiles, lane):
    turned = [turn(a, -1) for a in tiles]
    if len(tiles) == 1:
        return turned
    return [jnp.where(lane < L - 1, a, turned[(i + 1) % len(tiles)]) for i, a in enumerate(turned)]


def ring_west(tiles, lane):
    turned = [turn(a, 1) for a in tiles]
    if len(tiles) == 1:
        return turned
    return [jnp.where(lane > 0, a, turned[i - 1]) for i, a in enumerate(turned)]


def rows(at):
    return pl.ds(at, 8)


def kernel(
    ngy, ngx,
    tr_hbm, ea_hbm, no_hbm, co_hbm, th_hbm, sf_hbm, he_hbm,
    tr_out, h_out,
    th, a, ci, cf, s, c1, c2, c1s, c2s, fl, fls, me_s, mn_s, mes_s, mns_s, fx, fs,
    pw, pe, re, rw, v0_s, v1_s, v2_s, sh_s, inv_s, wet_s, row, b1, b2,
    load_sem, send_sem, recv_sem, rs_sem, rr_sem,
):
    f32 = jnp.float32
    gy, gx = lax.axis_index("gy"), lax.axis_index("gx")
    north, south = lax.rem(gy + 1, ngy), lax.rem(gy + ngy - 1, ngy)
    e_id, w_id = lax.rem(gx + 1, ngx), lax.rem(gx + ngx - 1, ngx)
    hi, z = lax.div(gx, 8), lax.rem(gx, 8)
    group1 = [
        (lax.rem(gy + dy, ngy), lax.rem(gx + 8 * dh, ngx))
        for dh in range(2) for dy in range(16) if dy or dh
    ]
    group2 = [(gy, hi * 8 + lax.rem(z + dz, 8)) for dz in range(1, 8)]
    near = [(north, gx), (south, gx), (gy, e_id), (gy, w_id),
            (north, e_id), (north, w_id), (south, e_id), (south, w_id)]

    own = pl.ds(8, R)
    halves = [pl.ds(0, L), pl.ds(L, L)]
    n_load = 0

    def load(src, dst):
        nonlocal n_load
        copy = pltpu.make_async_copy(src, dst, load_sem.at[n_load])
        n_load += 1
        copy.start()
        return copy

    level_loads = []
    for k in range(K):
        level_loads.append([
            load(src.at[k, :, half], a.at[base + k, i, own])
            for src, base in ((tr_hbm, TR), (ea_hbm, EA), (no_hbm, NO))
            for i, half in enumerate(halves)
        ])
    plane_loads = [
        load(src.at[:, half], dst.at[i, own])
        for src, dst in ((sf_hbm, a.at[SF]), (he_hbm, a.at[HE]), (co_hbm, ci))
        for i, half in enumerate(halves)
    ]
    th_load = load(th_hbm, th)

    barrier = pltpu.get_barrier_semaphore()
    for y, x in near + group1 + group2:
        pl.semaphore_signal(barrier, inc=1, device_id={"gy": y, "gx": x}, device_id_type=MESH)

    lane = lax.broadcasted_iota(jnp.int32, (8, L), 1)
    tiles = range(R // 8)

    packs = [[jnp.zeros((8, L), f32) for _ in tiles] for _ in range(2)]
    for group in range(K + 1):
        for copy in level_loads[group] if group < K else plane_loads:
            copy.wait()
        for field, at, first, last in PLAN[3 * group : 3 * group + 3]:
            for side in range(2):
                width = last if side else first
                start = at - 8 - width if side else at
                mask = window(lane, start, width)
                shift = at - 8 if side else at
                for t in tiles:
                    if field == CO:
                        value = ci[side, rows(8 + 8 * t), :].astype(f32)
                    else:
                        value = a[field, side, rows(8 + 8 * t), :]
                    packs[side][t] = jnp.where(mask, turn(value, shift), packs[side][t])
    for side, dest in enumerate((pw, pe)):
        for t in tiles:
            dest[rows(8 * t), :] = packs[side][t]

    pl.semaphore_wait(barrier, len(near) + len(group1) + len(group2))

    top, bottom = pl.ds(R + 3, HALO), pl.ds(8, HALO)
    ghost_s, ghost_n = pl.ds(3, HALO), pl.ds(R + 8, HALO)
    every, both = pl.ds(0, NF), pl.ds(0, 2)
    routes = [
        (pe, rw.at[own], (gy, e_id)),
        (pw, re.at[own], (gy, w_id)),
        (a.at[every, both, top], a.at[every, both, ghost_s], (north, gx)),
        (a.at[every, both, bottom], a.at[every, both, ghost_n], (south, gx)),
        (ci.at[both, top], ci.at[both, ghost_s], (north, gx)),
        (ci.at[both, bottom], ci.at[both, ghost_n], (south, gx)),
        (pe.at[pl.ds(R - HALO, HALO)], rw.at[ghost_s], (north, e_id)),
        (pw.at[pl.ds(R - HALO, HALO)], re.at[ghost_s], (north, w_id)),
        (pe.at[pl.ds(0, HALO)], rw.at[ghost_n], (south, e_id)),
        (pw.at[pl.ds(0, HALO)], re.at[ghost_n], (south, w_id)),
    ]
    sends = [
        pltpu.make_async_remote_copy(
            src_ref=src, dst_ref=dst, send_sem=send_sem.at[i], recv_sem=recv_sem.at[i],
            device_id={"gy": y, "gx": x}, device_id_type=MESH,
        )
        for i, (src, dst, (y, x)) in enumerate(routes)
    ]
    for copy in sends:
        copy.start()
    th_load.wait()

    def seam(field, at):
        left, right = (cf[0, rows(at), :], cf[1, rows(at), :]) if field == CO else (
            a[field, 0, rows(at), :], a[field, 1, rows(at), :])
        return jnp.where(lane < 64, turn(right, 4), turn(left, -4))

    for i in range(2):
        for t in tiles:
            at = 8 + 8 * t
            cf[i, rows(at), :] = ci[i, rows(at), :].astype(f32)
            fx[i, rows(at), :] = a[SF, i, rows(at), :]
    for field in range(NF + 1):
        for t in tiles:
            s[field, rows(8 + 8 * t), :] = seam(field, 8 + 8 * t)

    def face_masks(at, below):
        depth = [cf[i, rows(at), :] for i in range(2)]
        for i, other in enumerate(ring_east(depth, lane)):
            me_s[i, rows(at), :] = jnp.minimum(depth[i], other)
            mn_s[i, rows(below), :] = jnp.minimum(cf[i, rows(below), :], cf[i, rows(below + 1), :])

    for t in tiles:
        face_masks(8 + 8 * t, min(8 + 8 * t, R - 1))

    def north_flux(k, kf, i, current, at):
        speed = jnp.where(mn_s[i, rows(at), :] > kf, a[NO + k, i, rows(at), :], 0.0)
        return speed * jnp.where(speed > 0.0, current(i, at), current(i, at + 1))

    def east_flux(k, kf, now, at):
        out = []
        for i, other in enumerate(ring_east(now, lane)):
            speed = jnp.where(me_s[i, rows(at), :] > kf, a[EA + k, i, rows(at), :], 0.0)
            out.append(speed * jnp.where(speed > 0.0, now[i], other))
        return out

    def own_step(k, kf, current, store, starts, direct):
        if not direct:
            for at in [at - 1 for at in starts] + [starts[-1]]:
                for i in range(2):
                    fl[i, rows(at), :] = north_flux(k, kf, i, current, at)
        for at in starts:
            now = [current(i, at) for i in range(2)]
            fe = east_flux(k, kf, now, at)
            fw = ring_west(fe, lane)
            for i in range(2):
                if direct:
                    fn, fb = north_flux(k, kf, i, current, at), north_flux(k, kf, i, current, at - 1)
                else:
                    fn, fb = fl[i, rows(at), :], fl[i, rows(at - 1), :]
                store(i, at, now[i] - (fe[i] - fw[i] + fn - fb))

    def own_levels(k, starts1, starts2, direct):
        kf = k.astype(f32)
        weight = th[k]

        def put1(i, at, value):
            c1[k, i, rows(at), :] = value

        def put2(i, at, value):
            c2[k, i, rows(at), :] = value
            fx[i, rows(at), :] += jnp.where(cf[i, rows(at), :] > kf, weight * value, 0.0)

        own_step(k, kf, lambda i, at: a[TR + k, i, rows(at), :], put1, starts1, direct)
        own_step(k, kf, lambda i, at: c1[k, i, rows(at), :], put2, starts2, direct)

    starts1 = [9 + 8 * t for t in range(15)] + [R - 1]
    starts2 = [12 + 8 * t for t in range(15)]

    def interior(k, carry):
        own_levels(k, starts1, starts2, False)
        return carry

    lax.fori_loop(0, K, interior, 0)

    for copy in sends:
        copy.wait_recv()

    ghosts = window(lane, 4, HALO) | window(lane, 119, HALO)
    ends = (0, R + 8)
    for at in ends:
        for i in range(2):
            cf[i, rows(at), :] = ci[i, rows(at), :].astype(f32)
    zero8 = jnp.zeros((8, L), f32)

    for at0, edge in ((0, 0), (R + 8, ngy - 1)):

        @pl.when(gy == edge)
        def _(at0=at0):
            cf[0, rows(at0), :] = zero8
            cf[1, rows(at0), :] = zero8

    for field in range(NF + 1):
        for at in ends:
            s[field, rows(at), :] = seam(field, at)
    for first_row in (0, 48, 96):
        spots = [first_row + 8 * t for t in range(6)]
        from_east = [re[rows(at), :] for at in spots]
        from_west = [rw[rows(at), :] for at in spots]
        for field, at, first, _ in PLAN:
            mask = window(lane, at, first)
            for j, spot in enumerate(spots):
                value = turn(jnp.where(mask, from_east[j], from_west[j]), 4 - at)
                s[field, rows(spot), :] = jnp.where(ghosts, value, s[field, rows(spot), :])
    for at0, edge in ((0, 0), (R + 8, ngy - 1)):

        @pl.when(gy == edge)
        def _(at0=at0):
            s[CO, rows(at0), :] = zero8

    strips = (4, R + 4)
    for at in strips:
        face_masks(at, at - 1)
        for i in range(2):
            below = at + 1
            mn_s[i, rows(below), :] = jnp.minimum(cf[i, rows(below), :], cf[i, rows(below + 1), :])
            fx[i, rows(at), :] = a[SF, i, rows(at), :]
    seam_rows = [4 + 8 * t for t in range(17)]
    below_rows = [at - 1 for at in seam_rows] + [R + 11]
    for at in seam_rows:
        depth = s[CO, rows(at), :]
        mes_s[rows(at), :] = jnp.minimum(depth, turn(depth, -1))
        fs[rows(at), :] = s[SF, rows(at), :]
    for at in below_rows:
        mns_s[rows(at), :] = jnp.minimum(s[CO, rows(at), :], s[CO, rows(at + 1), :])

    def seam_step(k, j, kf, current, store):
        for at in below_rows:
            speed = jnp.where(mns_s[rows(at), :] > kf, s[NO + k, rows(at), :], 0.0)
            fls[j, rows(at), :] = speed * jnp.where(speed > 0.0, current(at), current(at + 1))
        for at in seam_rows:
            now = current(at)
            speed = jnp.where(mes_s[rows(at), :] > kf, s[EA + k, rows(at), :], 0.0)
            fe = speed * jnp.where(speed > 0.0, now, turn(now, -1))
            store(at, now - (fe - turn(fe, 1) + fls[j, rows(at), :] - fls[j, rows(at - 1), :]))

    def edges(step, carry):
        for j in range(UNROLL):
            k = step * UNROLL + j
            kf = k.astype(f32)
            weight = th[k]

            def put1(at, value, k=k):
                c1s[k, rows(at), :] = value

            def put2(at, value, k=k, kf=kf, weight=weight):
                c2s[k, rows(at), :] = value
                fs[rows(at), :] += jnp.where(s[CO, rows(at), :] > kf, weight * value, 0.0)

            seam_step(k, j, kf, lambda at, k=k: s[TR + k, rows(at), :], put1)
            seam_step(k, j, kf, lambda at, k=k: c1s[k, rows(at), :], put2)
            own_levels(k, strips, strips, True)
        return carry

    lax.fori_loop(0, K // UNROLL, edges, 0)

    blocks = [1] + [8 * t for t in range(1, 18)]
    inside = [8 * t for t in range(1, 17)]

    def beside(tile):
        return turn(tile, 4), turn(tile, -4)

    for at in blocks:
        f_w, f_e = beside(fs[rows(at), :])
        forcing = [
            jnp.where(lane < 2, f_w, fx[0, rows(at), :]),
            jnp.where(lane >= L - 2, f_e, fx[1, rows(at), :]),
            jnp.where(lane < 64, f_e, f_w),
        ]
        helm_w, helm_e = beside(s[HE, rows(at), :])
        helm = [a[HE, 0, rows(at), :], a[HE, 1, rows(at), :], jnp.where(lane < 64, helm_e, helm_w)]
        deep_w, deep_e = beside(s[CO, rows(at), :])
        deep = [cf[0, rows(at), :], cf[1, rows(at), :], jnp.where(lane < 64, deep_e, deep_w)]
        for i in range(3):
            inv = 1.0 / (6.0 + helm[i])
            inv_s[i, rows(at), :] = inv
            wet_s[i, rows(at), :] = jnp.where(deep[i] > 0.0, 1.0, 0.0)
            fx[i, rows(at), :] = forcing[i]
            v0_s[i, rows(at), :] = forcing[i] * inv

    nu = [[jnp.zeros((8, L), f32) for _ in range(2)] for _ in range(6)]

    def operator(n, src, spots, store):
        spread = {}
        for at in blocks:
            w = [src[i, rows(at), :] for i in range(3)]
            if n == 0:
                w = [wet_s[i, rows(at), :] * w[i] for i in range(3)]
            h = [x + y for x, y in zip(ring_west(w, lane), ring_east(w, lane))]
            spread[at] = h
            for i in range(3):
                sh_s[n, i, rows(at), :] = w[i] + 0.5 * h[i]
        for at in spots:
            for i in range(3):
                u = wet_s[i, rows(at), :] * (
                    spread[at][i] + sh_s[n, i, rows(at + 1), :] + sh_s[n, i, rows(at - 1), :])
                store(i, at, u)

    def counted(i, at):
        return i < 2 and at in inside

    def store1(i, at, u):
        v = u * inv_s[i, rows(at), :]
        v1_s[i, rows(at), :] = v
        if counted(i, at):
            f = fx[i, rows(at), :]
            nu[0][i] += f * v0_s[i, rows(at), :]
            nu[1][i] += v * f
            nu[2][i] += v * u

    def store2(i, at, u):
        v = u * inv_s[i, rows(at), :]
        v2_s[i, rows(at), :] = v
        if counted(i, at):
            nu[3][i] += v1_s[i, rows(at), :] * u
            nu[4][i] += v * u

    def store3(i, at, u):
        if counted(i, at):
            nu[5][i] += v2_s[i, rows(at), :] * u

    operator(0, v0_s, blocks, store1)
    operator(1, v1_s, blocks, store2)
    operator(2, v2_s, inside, store3)

    def finish_tracer():
        def put(k, carry):
            for t in tiles:
                at = 8 + 8 * t
                turned = beside(c2s[k, rows(at), :])
                for i, mask in enumerate((lane < 2, lane >= L - 2)):
                    tr_out[k, rows(8 * t), halves[i]] = jnp.where(mask, turned[i], c2[k, i, rows(at), :])
            return carry

        lax.fori_loop(0, K, put, 0)

    lane1 = lax.broadcasted_iota(jnp.int32, (1, 128), 1)
    packed = jnp.zeros((1, 128), jnp.float32)
    for i, part in enumerate(nu):
        lanes = jnp.sum(part[0] + part[1], axis=0, keepdims=True)
        total = jnp.sum(lanes, axis=1, keepdims=True)
        packed = jnp.where(lane1 == i, total, packed)

    reduce_sends = []
    for i, (group, slot, buf) in enumerate(((group1, gy * 2 + hi, b1), (group2, z, b2))):
        row[i] = packed
        n = len(group)
        for y, x in group:
            copy = pltpu.make_async_remote_copy(
                src_ref=row.at[i], dst_ref=buf.at[slot], send_sem=rs_sem.at[i], recv_sem=rr_sem.at[i],
                device_id={"gy": y, "gx": x}, device_id_type=MESH,
            )
            copy.start()
        buf[slot] = packed
        if i == 0:
            finish_tracer()
        pltpu.make_async_copy(buf.at[pl.ds(0, n)], buf.at[pl.ds(0, n)], rr_sem.at[i]).wait()
        reduce_sends.append((buf, n, i))
        packed = jnp.sum(buf[...], axis=0)

    m = [jnp.sum(jnp.where(lane1 == i, packed, 0.0), axis=1, keepdims=True) for i in range(6)]

    def form(p, moments):
        total = None
        for i, pi in enumerate(p):
            for j, pj in enumerate(p[i:], i):
                term = (pi * pj if i == j else 2.0 * pi * pj) * moments[i + j]
                total = term if total is None else total + term
        return total

    diff = [m[i] - m[i + 1] for i in range(5)]
    one = jnp.ones_like(m[0])
    zc, pc = [one], [one]
    heights = [jnp.zeros_like(one)] * 3
    rz = m[0]
    for it in range(ITERS):
        alpha = rz / form(pc, diff)
        heights = [h + alpha * pc[i] if i < len(pc) else h for i, h in enumerate(heights)]
        if it + 1 < ITERS:
            applied = [p - q for p, q in zip(pc + [jnp.zeros_like(one)], [jnp.zeros_like(one)] + pc)]
            zc = [(zc[i] if i < len(zc) else 0.0) - alpha * applied[i] for i in range(len(applied))]
            rz_next = form(zc, m)
            beta = rz_next / rz
            pc = [zc[i] + beta * pc[i] if i < len(pc) else zc[i] for i in range(len(zc))]
            rz = rz_next

    for t in tiles:
        at = 8 + 8 * t
        for i in range(2):
            h_out[rows(8 * t), halves[i]] = (
                heights[0] * v0_s[i, rows(at), :] + heights[1] * v1_s[i, rows(at), :] + heights[2] * v2_s[i, rows(at), :])

    for copy in sends:
        copy.wait_send()
    for buf, n, i in reduce_sends:
        pltpu.make_async_copy(buf.at[pl.ds(0, n)], buf.at[pl.ds(0, n)], rs_sem.at[i]).wait()


def put_kernel(tr, h, tr_hbm, h_hbm, sem):
    copies = [pltpu.make_async_copy(tr, tr_hbm, sem.at[0]), pltpu.make_async_copy(h, h_hbm, sem.at[1])]
    for copy in copies:
        copy.start()
    for copy in copies:
        copy.wait()


def on_device(ngy, ngx, tracer, east_speed, north_speed, columns, thickness, surface_flux, helm):
    f32 = jnp.float32
    any_spec = pl.BlockSpec(memory_space=pltpu.HBM)
    vmem = pl.BlockSpec(memory_space=pltpu.VMEM)
    results = pl.pallas_call(
        functools.partial(kernel, ngy, ngx),
        out_shape=(pltpu.VMEM((K, R, C), f32), pltpu.VMEM((R, C), f32)),
        in_specs=[any_spec, any_spec, any_spec, any_spec, any_spec, any_spec, any_spec],
        out_specs=(vmem, vmem),
        scratch_shapes=[
            pltpu.SMEM((K,), f32),
            pltpu.VMEM((NF, 2, RE, L), f32),
            pltpu.VMEM((2, RE, L), jnp.int32),
            pltpu.VMEM((2, RE, L), f32),
            pltpu.VMEM((NF + 1, RE, L), f32),
            pltpu.VMEM((K, 2, RE, L), f32),
            pltpu.VMEM((K, 2, RE, L), f32),
            pltpu.VMEM((K, RE, L), f32),
            pltpu.VMEM((K, RE, L), f32),
            pltpu.VMEM((2, RE, L), f32),
            pltpu.VMEM((UNROLL, RE, L), f32),
            pltpu.VMEM((2, RE, L), f32),
            pltpu.VMEM((2, RE, L), f32),
            pltpu.VMEM((RE, L), f32),
            pltpu.VMEM((RE, L), f32),
            pltpu.VMEM((3, RE, L), f32),
            pltpu.VMEM((RE, L), f32),
            pltpu.VMEM((R, L), f32),
            pltpu.VMEM((R, L), f32),
            pltpu.VMEM((RE, L), f32),
            pltpu.VMEM((RE, L), f32),
            pltpu.VMEM((3, RE, L), f32),
            pltpu.VMEM((3, RE, L), f32),
            pltpu.VMEM((3, RE, L), f32),
            pltpu.VMEM((3, 3, RE, L), f32),
            pltpu.VMEM((3, RE, L), f32),
            pltpu.VMEM((3, RE, L), f32),
            pltpu.VMEM((2, 1, L), f32),
            pltpu.VMEM((32, 1, L), f32),
            pltpu.VMEM((8, 1, L), f32),
            pltpu.SemaphoreType.DMA((6 * K + 7,)),
            pltpu.SemaphoreType.DMA((10,)),
            pltpu.SemaphoreType.DMA((10,)),
            pltpu.SemaphoreType.DMA((2,)),
            pltpu.SemaphoreType.DMA((2,)),
        ],
        compiler_params=pltpu.CompilerParams(collective_id=0, has_side_effects=True),
    )(tracer, east_speed, north_speed, columns, thickness, surface_flux, helm)
    return pl.pallas_call(
        put_kernel,
        out_shape=(jax.ShapeDtypeStruct((K, R, C), f32), jax.ShapeDtypeStruct((R, C), f32)),
        in_specs=[vmem, vmem],
        out_specs=(any_spec, any_spec),
        scratch_shapes=[pltpu.SemaphoreType.DMA((2,))],
    )(*[pltpu.with_memory_space_constraint(r, pltpu.VMEM) for r in results])


def solution(mesh):
    sizes = mesh.shape
    cells, plane = P(None, "gy", "gx"), P("gy", "gx")
    return jax.shard_map(
        functools.partial(on_device, sizes["gy"], sizes["gx"]),
        mesh=mesh,
        in_specs=(cells, cells, cells, plane, P(), plane, plane),
        out_specs=(cells, plane),
        check_vma=False,
    )
```

time: 31.5 us -> 29.7 us (0.943)
  Pallas kernels: 30.8 us -> 29 us
    pallas_call x1, Pallas kernels: 29.8 us -> 28 us  [on_device(): pl.pallas_call(functools.partial(kernel, ngy, ngx), out_shape=(pltpu.VMEM...]
where the time goes in v3:
time: 29.7 us; the launch traced here: 29.6 us
  Pallas kernels  29 us (98%)
  between operations  0.64 us (2%)
    pallas_call x1, Pallas kernels, on_device(): pl.pallas_call(functools.partial(kernel, ngy, ngx), out_shape=(pltpu.VMEM...  28 us
    pallas_call x1, Pallas kernels, on_device(): pl.pallas_call(put_kernel, out_shape=(jax.ShapeDtypeStruct((K, R, C), f32...  1.02 us

profile of v3, /device:TPU:1, one launch (start us, length us, event | category | flops | bytes accessed | tf_op | source)
XLA Modules:
  0.0 29.6 jit_solution(17975270897124554269)
XLA Ops:
  0.6 28.0 %shard_map.86 = (f32[8,128,256]{2,1,0:T(8,128)S(1)}, f32[128,256]{1,0:T(8,128)S(1)}) custom-call(f32[8,128,256]{2,1,0:T(8,128)} %tr_hbm.1, f32[8,128,256]{2,1,0:T(8,128)} %ea_hbm.1, f32[8,128,256]{2,1,0:T(8,128)} %no_hbm.1, s32[128,256]{1,0:T(8,128)} %co_hbm.1, f32[8]{0:T(128)} %th_hbm.1, f32[128,256]{1,0:T(8,128)} %sf_hbm.1, f32[128,256]{1,0:T(8,128)} %he_hbm.1), custom_call_target="tpu_custom_call" | custom-call | tf_op jit(solution)/shard_map/pallas_call | solution.py:477
  28.6 1.0 %shard_map.87 = (f32[8,128,256]{2,1,0:T(8,128)}, f32[128,256]{1,0:T(8,128)}) custom-call(f32[8,128,256]{2,1,0:T(8,128)S(1)} %get-tuple-element.4.tr, f32[128,256]{1,0:T(8,128)S(1)} %get-tuple-element.5.h), custom_call_target="tpu_custom_call" | custom-call | tf_op jit(solution)/shard_map/pallas_call | solution.py:521

commit v4 on v3

--- a/solution.py
+++ b/solution.py
@@ -10,12 +10,14 @@
 ITERS = 3
 K = 8
 R, C, L = 128, 256, 128
-RE = R + 24
+RE = R + 32
 HALO = 5
 MESH = pl.DeviceIdType.MESH
 TR, EA, NO, SF, HE, CO = 0, K, 2 * K, 3 * K, 3 * K + 1, 3 * K + 2
 NF = 3 * K + 2
-UNROLL = 2
+UNROLL = 4
+STRIP_UNROLL = 4
+PAIR = 2
 
 
 def lane_plan():
@@ -82,47 +84,43 @@
         (lax.rem(gy + dy, ngy), lax.rem(gx + 8 * dh, ngx))
         for dh in range(2) for dy in range(16) if dy or dh
     ]
+    far1 = [device for i, device in enumerate(group1) if i not in (0, 14)]
     group2 = [(gy, hi * 8 + lax.rem(z + dz, 8)) for dz in range(1, 8)]
     near = [(north, gx), (south, gx), (gy, e_id), (gy, w_id),
             (north, e_id), (north, w_id), (south, e_id), (south, w_id)]
 
-    own = pl.ds(8, R)
+    barrier = pltpu.get_barrier_semaphore()
+
+    def greet(devices):
+        for y, x in devices:
+            pl.semaphore_signal(barrier, inc=1, device_id={"gy": y, "gx": x}, device_id_type=MESH)
+
+    greet(near)
+    own, both = pl.ds(8, R), pl.ds(0, 2)
     halves = [pl.ds(0, L), pl.ds(L, L)]
-    n_load = 0
-
-    def load(src, dst):
-        nonlocal n_load
-        copy = pltpu.make_async_copy(src, dst, load_sem.at[n_load])
-        n_load += 1
-        copy.start()
-        return copy
-
-    level_loads = []
-    for k in range(K):
-        level_loads.append([
-            load(src.at[k, :, half], a.at[base + k, i, own])
-            for src, base in ((tr_hbm, TR), (ea_hbm, EA), (no_hbm, NO))
-            for i, half in enumerate(halves)
-        ])
-    plane_loads = [
-        load(src.at[:, half], dst.at[i, own])
-        for src, dst in ((sf_hbm, a.at[SF]), (he_hbm, a.at[HE]), (co_hbm, ci))
-        for i, half in enumerate(halves)
-    ]
-    th_load = load(th_hbm, th)
-
-    barrier = pltpu.get_barrier_semaphore()
-    for y, x in near + group1 + group2:
-        pl.semaphore_signal(barrier, inc=1, device_id={"gy": y, "gx": x}, device_id_type=MESH)
+    for g in range(K // PAIR):
+        for src, base in ((tr_hbm, TR), (ea_hbm, EA), (no_hbm, NO)):
+            for i, half in enumerate(halves):
+                pltpu.make_async_copy(
+                    src.at[pl.ds(PAIR * g, PAIR), :, half], a.at[pl.ds(base + PAIR * g, PAIR), i, own], load_sem.at[g]
+                ).start()
+    for src, dst in ((sf_hbm, a.at[SF]), (he_hbm, a.at[HE]), (co_hbm, ci)):
+        for i, half in enumerate(halves):
+            pltpu.make_async_copy(src.at[:, half], dst.at[i, own], load_sem.at[K // PAIR]).start()
+    th_load = pltpu.make_async_copy(th_hbm, th, load_sem.at[K // PAIR + 1])
+    th_load.start()
+    greet(far1 + group2)
+
+    def wait_rows(ref, sem):
+        pltpu.make_async_copy(ref, ref, sem).wait()
 
     lane = lax.broadcasted_iota(jnp.int32, (8, L), 1)
     tiles = range(R // 8)
 
     packs = [[jnp.zeros((8, L), f32) for _ in tiles] for _ in range(2)]
-    for group in range(K + 1):
-        for copy in level_loads[group] if group < K else plane_loads:
-            copy.wait()
-        for field, at, first, last in PLAN[3 * group : 3 * group + 3]:
+    for g in range(K // PAIR + 1):
+        wait_rows(a.at[pl.ds(0, 3 * PAIR if g < K // PAIR else 3), both, own], load_sem.at[g])
+        for field, at, first, last in PLAN[3 * PAIR * g : 3 * PAIR * (g + 1)]:
             for side in range(2):
                 width = last if side else first
                 start = at - 8 - width if side else at
@@ -138,44 +136,54 @@
         for t in tiles:
             dest[rows(8 * t), :] = packs[side][t]
 
-    pl.semaphore_wait(barrier, len(near) + len(group1) + len(group2))
+    pl.semaphore_wait(barrier, len(near) + len(far1) + len(group2))
 
     top, bottom = pl.ds(R + 3, HALO), pl.ds(8, HALO)
     ghost_s, ghost_n = pl.ds(3, HALO), pl.ds(R + 8, HALO)
-    every, both = pl.ds(0, NF), pl.ds(0, 2)
+    every = pl.ds(0, NF)
     routes = [
-        (pe, rw.at[own], (gy, e_id)),
-        (pw, re.at[own], (gy, w_id)),
-        (a.at[every, both, top], a.at[every, both, ghost_s], (north, gx)),
-        (a.at[every, both, bottom], a.at[every, both, ghost_n], (south, gx)),
-        (ci.at[both, top], ci.at[both, ghost_s], (north, gx)),
-        (ci.at[both, bottom], ci.at[both, ghost_n], (south, gx)),
-        (pe.at[pl.ds(R - HALO, HALO)], rw.at[ghost_s], (north, e_id)),
-        (pw.at[pl.ds(R - HALO, HALO)], re.at[ghost_s], (north, w_id)),
-        (pe.at[pl.ds(0, HALO)], rw.at[ghost_n], (south, e_id)),
-        (pw.at[pl.ds(0, HALO)], re.at[ghost_n], (south, w_id)),
+        (0, pe.at[pl.ds(R - HALO, HALO)], rw.at[ghost_s], (north, e_id)),
+        (0, pw.at[pl.ds(R - HALO, HALO)], re.at[ghost_s], (north, w_id)),
+        (0, pe.at[pl.ds(0, HALO)], rw.at[ghost_n], (south, e_id)),
+        (0, pw.at[pl.ds(0, HALO)], re.at[ghost_n], (south, w_id)),
+        (0, pe, rw.at[own], (gy, e_id)),
+        (0, pw, re.at[own], (gy, w_id)),
+        (1, ci.at[both, top], ci.at[both, ghost_s], (north, gx)),
+        (1, ci.at[both, bottom], ci.at[both, ghost_n], (south, gx)),
+        (1, a.at[every, both, top], a.at[every, both, ghost_s], (north, gx)),
+        (1, a.at[every, both, bottom], a.at[every, both, ghost_n], (south, gx)),
     ]
-    sends = [
+    for kind, src, dst, (y, x) in routes:
         pltpu.make_async_remote_copy(
-            src_ref=src, dst_ref=dst, send_sem=send_sem.at[i], recv_sem=recv_sem.at[i],
+            src_ref=src, dst_ref=dst, send_sem=send_sem, recv_sem=recv_sem.at[kind],
             device_id={"gy": y, "gx": x}, device_id_type=MESH,
-        )
-        for i, (src, dst, (y, x)) in enumerate(routes)
-    ]
-    for copy in sends:
-        copy.start()
+        ).start()
+    column_rows = (1, 2, R + 2 * HALO)
+    row_rows = (2, 2, 5 * (NF + 1))
+    sent_rows = (3, 2, 136)
+    assert 2 * (R + 2 * HALO) == 2 * R + 4 * HALO and 4 * 5 * (NF + 1) == 2 * 2 * HALO * (NF + 1)
+    assert 6 * 136 == 2 * (R + 2 * HALO) + 20 * (NF + 1)
+
+    def sized(shape):
+        return c1.at[pl.ds(0, shape[0]), pl.ds(0, shape[1]), pl.ds(0, shape[2])]
+
     th_load.wait()
 
     def seam(field, at):
         left, right = (cf[0, rows(at), :], cf[1, rows(at), :]) if field == CO else (
             a[field, 0, rows(at), :], a[field, 1, rows(at), :])
         return jnp.where(lane < 64, turn(right, 4), turn(left, -4))
+
+    def diagonal(i, at, helm, depth):
+        inv_s[i, rows(at), :] = 1.0 / (6.0 + helm)
+        wet_s[i, rows(at), :] = jnp.where(depth > 0.0, 1.0, 0.0)
 
     for i in range(2):
         for t in tiles:
             at = 8 + 8 * t
             cf[i, rows(at), :] = ci[i, rows(at), :].astype(f32)
             fx[i, rows(at), :] = a[SF, i, rows(at), :]
+            diagonal(i, at, a[HE, i, rows(at), :], cf[i, rows(at), :])
     for field in range(NF + 1):
         for t in tiles:
             s[field, rows(8 + 8 * t), :] = seam(field, 8 + 8 * t)
@@ -239,26 +247,10 @@
 
     lax.fori_loop(0, K, interior, 0)
 
-    for copy in sends:
-        copy.wait_recv()
+    wait_rows(sized(column_rows), recv_sem.at[0])
 
     ghosts = window(lane, 4, HALO) | window(lane, 119, HALO)
     ends = (0, R + 8)
-    for at in ends:
-        for i in range(2):
-            cf[i, rows(at), :] = ci[i, rows(at), :].astype(f32)
-    zero8 = jnp.zeros((8, L), f32)
-
-    for at0, edge in ((0, 0), (R + 8, ngy - 1)):
-
-        @pl.when(gy == edge)
-        def _(at0=at0):
-            cf[0, rows(at0), :] = zero8
-            cf[1, rows(at0), :] = zero8
-
-    for field in range(NF + 1):
-        for at in ends:
-            s[field, rows(at), :] = seam(field, at)
     for first_row in (0, 48, 96):
         spots = [first_row + 8 * t for t in range(6)]
         from_east = [re[rows(at), :] for at in spots]
@@ -267,64 +259,114 @@
             mask = window(lane, at, first)
             for j, spot in enumerate(spots):
                 value = turn(jnp.where(mask, from_east[j], from_west[j]), 4 - at)
-                s[field, rows(spot), :] = jnp.where(ghosts, value, s[field, rows(spot), :])
-    for at0, edge in ((0, 0), (R + 8, ngy - 1)):
-
-        @pl.when(gy == edge)
-        def _(at0=at0):
-            s[CO, rows(at0), :] = zero8
+                if spot not in ends:
+                    value = jnp.where(ghosts, value, s[field, rows(spot), :])
+                s[field, rows(spot), :] = value
+
+    def beside(tile):
+        return turn(tile, 4), turn(tile, -4)
+
+    def ghost_tile(field, at):
+        west, east = beside(s[field, rows(at), :])
+        return jnp.where(lane < 64, east, west)
+
+    for t in tiles:
+        at = 8 + 8 * t
+        depth = s[CO, rows(at), :]
+        mes_s[rows(at), :] = jnp.minimum(depth, turn(depth, -1))
+        below = min(at, R - 1)
+        mns_s[rows(below), :] = jnp.minimum(s[CO, rows(below), :], s[CO, rows(below + 1), :])
+        fs[rows(at), :] = s[SF, rows(at), :]
+        diagonal(2, at, ghost_tile(HE, at), ghost_tile(CO, at))
+
+    def seam_flux(k, kf, current, at):
+        speed = jnp.where(mns_s[rows(at), :] > kf, s[NO + k, rows(at), :], 0.0)
+        return speed * jnp.where(speed > 0.0, current(at), current(at + 1))
+
+    def seam_step(k, j, kf, current, store, starts, direct):
+        if not direct:
+            for at in [at - 1 for at in starts] + [starts[-1]]:
+                fls[j, rows(at), :] = seam_flux(k, kf, current, at)
+        for at in starts:
+            now = current(at)
+            speed = jnp.where(mes_s[rows(at), :] > kf, s[EA + k, rows(at), :], 0.0)
+            fe = speed * jnp.where(speed > 0.0, now, turn(now, -1))
+            if direct:
+                fn, fb = seam_flux(k, kf, current, at), seam_flux(k, kf, current, at - 1)
+            else:
+                fn, fb = fls[j, rows(at), :], fls[j, rows(at - 1), :]
+            store(at, now - (fe - turn(fe, 1) + fn - fb))
+
+    def seam_levels(k, j, starts1, starts2, direct):
+        kf = k.astype(f32)
+        weight = th[k]
+
+        def put1(at, value):
+            c1s[k, rows(at), :] = value
+
+        def put2(at, value):
+            c2s[k, rows(at), :] = value
+            fs[rows(at), :] += jnp.where(s[CO, rows(at), :] > kf, weight * value, 0.0)
+
+        seam_step(k, j, kf, lambda at: s[TR + k, rows(at), :], put1, starts1, direct)
+        seam_step(k, j, kf, lambda at: c1s[k, rows(at), :], put2, starts2, direct)
+
+    def seams(step, carry):
+        for j in range(UNROLL):
+            seam_levels(step * UNROLL + j, j, starts1, starts2, False)
+        return carry
+
+    lax.fori_loop(0, K // UNROLL, seams, 0)
+
+    wait_rows(sized(row_rows), recv_sem.at[1])
+
+    zero8 = jnp.zeros((8, L), f32)
+    for at in ends:
+        for i in range(2):
+            cf[i, rows(at), :] = ci[i, rows(at), :].astype(f32)
+
+    def shut():
+        for at0, edge in ((0, 0), (R + 8, ngy - 1)):
+
+            @pl.when(gy == edge)
+            def _(at0=at0):
+                cf[0, rows(at0), :] = zero8
+                cf[1, rows(at0), :] = zero8
+                s[CO, rows(at0), :] = zero8
+
+    for field in range(NF + 1):
+        for at in ends:
+            s[field, rows(at), :] = jnp.where(ghosts, s[field, rows(at), :], seam(field, at))
+    shut()
 
     strips = (4, R + 4)
     for at in strips:
         face_masks(at, at - 1)
+        below = at + 1
         for i in range(2):
-            below = at + 1
             mn_s[i, rows(below), :] = jnp.minimum(cf[i, rows(below), :], cf[i, rows(below + 1), :])
             fx[i, rows(at), :] = a[SF, i, rows(at), :]
-    seam_rows = [4 + 8 * t for t in range(17)]
-    below_rows = [at - 1 for at in seam_rows] + [R + 11]
-    for at in seam_rows:
         depth = s[CO, rows(at), :]
         mes_s[rows(at), :] = jnp.minimum(depth, turn(depth, -1))
+        for below in (at - 1, at + 1):
+            mns_s[rows(below), :] = jnp.minimum(s[CO, rows(below), :], s[CO, rows(below + 1), :])
         fs[rows(at), :] = s[SF, rows(at), :]
-    for at in below_rows:
-        mns_s[rows(at), :] = jnp.minimum(s[CO, rows(at), :], s[CO, rows(at + 1), :])
-
-    def seam_step(k, j, kf, current, store):
-        for at in below_rows:
-            speed = jnp.where(mns_s[rows(at), :] > kf, s[NO + k, rows(at), :], 0.0)
-            fls[j, rows(at), :] = speed * jnp.where(speed > 0.0, current(at), current(at + 1))
-        for at in seam_rows:
-            now = current(at)
-            speed = jnp.where(mes_s[rows(at), :] > kf, s[EA + k, rows(at), :], 0.0)
-            fe = speed * jnp.where(speed > 0.0, now, turn(now, -1))
-            store(at, now - (fe - turn(fe, 1) + fls[j, rows(at), :] - fls[j, rows(at - 1), :]))
+    for at in ends:
+        for i in range(2):
+            diagonal(i, at, a[HE, i, rows(at), :], cf[i, rows(at), :])
+        diagonal(2, at, ghost_tile(HE, at), ghost_tile(CO, at))
 
     def edges(step, carry):
-        for j in range(UNROLL):
-            k = step * UNROLL + j
-            kf = k.astype(f32)
-            weight = th[k]
-
-            def put1(at, value, k=k):
-                c1s[k, rows(at), :] = value
-
-            def put2(at, value, k=k, kf=kf, weight=weight):
-                c2s[k, rows(at), :] = value
-                fs[rows(at), :] += jnp.where(s[CO, rows(at), :] > kf, weight * value, 0.0)
-
-            seam_step(k, j, kf, lambda at, k=k: s[TR + k, rows(at), :], put1)
-            seam_step(k, j, kf, lambda at, k=k: c1s[k, rows(at), :], put2)
+        for j in range(STRIP_UNROLL):
+            k = step * STRIP_UNROLL + j
             own_levels(k, strips, strips, True)
+            seam_levels(k, j, strips, strips, True)
         return carry
 
-    lax.fori_loop(0, K // UNROLL, edges, 0)
+    lax.fori_loop(0, K // STRIP_UNROLL, edges, 0)
 
     blocks = [1] + [8 * t for t in range(1, 18)]
     inside = [8 * t for t in range(1, 17)]
-
-    def beside(tile):
-        return turn(tile, 4), turn(tile, -4)
 
     for at in blocks:
         f_w, f_e = beside(fs[rows(at), :])
@@ -333,16 +375,9 @@
             jnp.where(lane >= L - 2, f_e, fx[1, rows(at), :]),
             jnp.where(lane < 64, f_e, f_w),
         ]
-        helm_w, helm_e = beside(s[HE, rows(at), :])
-        helm = [a[HE, 0, rows(at), :], a[HE, 1, rows(at), :], jnp.where(lane < 64, helm_e, helm_w)]
-        deep_w, deep_e = beside(s[CO, rows(at), :])
-        deep = [cf[0, rows(at), :], cf[1, rows(at), :], jnp.where(lane < 64, deep_e, deep_w)]
         for i in range(3):
-            inv = 1.0 / (6.0 + helm[i])
-            inv_s[i, rows(at), :] = inv
-            wet_s[i, rows(at), :] = jnp.where(deep[i] > 0.0, 1.0, 0.0)
             fx[i, rows(at), :] = forcing[i]
-            v0_s[i, rows(at), :] = forcing[i] * inv
+            v0_s[i, rows(at), :] = forcing[i] * inv_s[i, rows(at), :]
 
     nu = [[jnp.zeros((8, L), f32) for _ in range(2)] for _ in range(6)]
 
@@ -456,8 +491,7 @@
             h_out[rows(8 * t), halves[i]] = (
                 heights[0] * v0_s[i, rows(at), :] + heights[1] * v1_s[i, rows(at), :] + heights[2] * v2_s[i, rows(at), :])
 
-    for copy in sends:
-        copy.wait_send()
+    wait_rows(sized(sent_rows), send_sem)
     for buf, n, i in reduce_sends:
         pltpu.make_async_copy(buf.at[pl.ds(0, n)], buf.at[pl.ds(0, n)], rs_sem.at[i]).wait()
 
@@ -510,9 +544,9 @@
             pltpu.VMEM((2, 1, L), f32),
             pltpu.VMEM((32, 1, L), f32),
             pltpu.VMEM((8, 1, L), f32),
-            pltpu.SemaphoreType.DMA((6 * K + 7,)),
-            pltpu.SemaphoreType.DMA((10,)),
-            pltpu.SemaphoreType.DMA((10,)),
+            pltpu.SemaphoreType.DMA((K // PAIR + 2,)),
+            pltpu.SemaphoreType.DMA,
+            pltpu.SemaphoreType.DMA((2,)),
             pltpu.SemaphoreType.DMA((2,)),
             pltpu.SemaphoreType.DMA((2,)),
         ],

time: 29.7 us -> 29.1 us (0.980)
  Pallas kernels: 29 us -> 28.4 us
    pallas_call x1, Pallas kernels: 28 us -> 27.4 us  [on_device(): pl.pallas_call(functools.partial(kernel, ngy, ngx), out_shape=(pltpu.VMEM...]
where the time goes in v4:
time: 29.1 us; the launch traced here: 29 us
  Pallas kernels  28.4 us (98%)
  between operations  0.64 us (2%)
    pallas_call x1, Pallas kernels, on_device(): pl.pallas_call(functools.partial(kernel, ngy, ngx), out_shape=(pltpu.VMEM...  27.4 us
    pallas_call x1, Pallas kernels, on_device(): pl.pallas_call(put_kernel, out_shape=(jax.ShapeDtypeStruct((K, R, C), f32...  1.02 us

profile of v4, /device:TPU:1, one launch (start us, length us, event | category | flops | bytes accessed | tf_op | source)
XLA Modules:
  0.0 29.0 jit_solution(6252745603751733232)
XLA Ops:
  0.6 27.4 %shard_map.86 = (f32[8,128,256]{2,1,0:T(8,128)S(1)}, f32[128,256]{1,0:T(8,128)S(1)}) custom-call(f32[8,128,256]{2,1,0:T(8,128)} %tr_hbm.1, f32[8,128,256]{2,1,0:T(8,128)} %ea_hbm.1, f32[8,128,256]{2,1,0:T(8,128)} %no_hbm.1, s32[128,256]{1,0:T(8,128)} %co_hbm.1, f32[8]{0:T(128)} %th_hbm.1, f32[128,256]{1,0:T(8,128)} %sf_hbm.1, f32[128,256]{1,0:T(8,128)} %he_hbm.1), custom_call_target="tpu_custom_call" | custom-call | tf_op jit(solution)/shard_map/pallas_call | solution.py:511
  28.0 1.0 %shard_map.87 = (f32[8,128,256]{2,1,0:T(8,128)}, f32[128,256]{1,0:T(8,128)}) custom-call(f32[8,128,256]{2,1,0:T(8,128)S(1)} %get-tuple-element.4.tr, f32[128,256]{1,0:T(8,128)S(1)} %get-tuple-element.5.h), custom_call_target="tpu_custom_call" | custom-call | tf_op jit(solution)/shard_map/pallas_call | solution.py:555

commit v5 on v4

--- a/solution.py
+++ b/solution.py
@@ -10,13 +10,13 @@
 ITERS = 3
 K = 8
 R, C, L = 128, 256, 128
-RE = R + 32
+RE = R + 24
 HALO = 5
 MESH = pl.DeviceIdType.MESH
 TR, EA, NO, SF, HE, CO = 0, K, 2 * K, 3 * K, 3 * K + 1, 3 * K + 2
 NF = 3 * K + 2
 UNROLL = 4
-STRIP_UNROLL = 4
+STRIP_UNROLL = 8
 PAIR = 2
 
 
@@ -141,31 +141,65 @@
     top, bottom = pl.ds(R + 3, HALO), pl.ds(8, HALO)
     ghost_s, ghost_n = pl.ds(3, HALO), pl.ds(R + 8, HALO)
     every = pl.ds(0, NF)
-    routes = [
-        (0, pe.at[pl.ds(R - HALO, HALO)], rw.at[ghost_s], (north, e_id)),
-        (0, pw.at[pl.ds(R - HALO, HALO)], re.at[ghost_s], (north, w_id)),
-        (0, pe.at[pl.ds(0, HALO)], rw.at[ghost_n], (south, e_id)),
-        (0, pw.at[pl.ds(0, HALO)], re.at[ghost_n], (south, w_id)),
-        (0, pe, rw.at[own], (gy, e_id)),
-        (0, pw, re.at[own], (gy, w_id)),
-        (1, ci.at[both, top], ci.at[both, ghost_s], (north, gx)),
-        (1, ci.at[both, bottom], ci.at[both, ghost_n], (south, gx)),
-        (1, a.at[every, both, top], a.at[every, both, ghost_s], (north, gx)),
-        (1, a.at[every, both, bottom], a.at[every, both, ghost_n], (south, gx)),
-    ]
-    for kind, src, dst, (y, x) in routes:
+
+    def send(kind, src, dst, y, x):
         pltpu.make_async_remote_copy(
-            src_ref=src, dst_ref=dst, send_sem=send_sem, recv_sem=recv_sem.at[kind],
+            src_ref=src, dst_ref=dst, send_sem=send_sem.at[kind], recv_sem=recv_sem.at[kind],
             device_id={"gy": y, "gx": x}, device_id_type=MESH,
         ).start()
-    column_rows = (1, 2, R + 2 * HALO)
-    row_rows = (2, 2, 5 * (NF + 1))
-    sent_rows = (3, 2, 136)
-    assert 2 * (R + 2 * HALO) == 2 * R + 4 * HALO and 4 * 5 * (NF + 1) == 2 * 2 * HALO * (NF + 1)
-    assert 6 * 136 == 2 * (R + 2 * HALO) + 20 * (NF + 1)
+
+    has_north, has_south = gy < ngy - 1, gy > 0
+
+    @pl.when(has_north)
+    def _():
+        send(1, pe.at[pl.ds(R - HALO, HALO)], rw.at[ghost_s], north, e_id)
+        send(1, pw.at[pl.ds(R - HALO, HALO)], re.at[ghost_s], north, w_id)
+
+    @pl.when(has_south)
+    def _():
+        send(2, pe.at[pl.ds(0, HALO)], rw.at[ghost_n], south, e_id)
+        send(2, pw.at[pl.ds(0, HALO)], re.at[ghost_n], south, w_id)
+
+    send(0, pe, rw.at[own], gy, e_id)
+    send(0, pw, re.at[own], gy, w_id)
+
+    @pl.when(has_north)
+    def _():
+        send(1, ci.at[both, top], ci.at[both, ghost_s], north, gx)
+        send(1, a.at[every, both, top], a.at[every, both, ghost_s], north, gx)
+
+    @pl.when(has_south)
+    def _():
+        send(2, ci.at[both, bottom], ci.at[both, ghost_n], south, gx)
+        send(2, a.at[every, both, bottom], a.at[every, both, ghost_n], south, gx)
+
+    column_rows = (1, 2, R)
+    row_rows = (1, 2, HALO * (NF + 2))
+    assert RE >= HALO * (NF + 2)
 
     def sized(shape):
         return c1.at[pl.ds(0, shape[0]), pl.ds(0, shape[1]), pl.ds(0, shape[2])]
+
+    def each_end(sem):
+        @pl.when(has_north if sem is send_sem else has_south)
+        def _():
+            wait_rows(sized(row_rows), sem.at[1])
+
+        @pl.when(has_south if sem is send_sem else has_north)
+        def _():
+            wait_rows(sized(row_rows), sem.at[2])
+
+    zero8 = jnp.zeros((8, L), f32)
+    for at0, open_end in ((0, has_south), (R + 8, has_north)):
+
+        @pl.when(jnp.logical_not(open_end))
+        def _(at0=at0):
+            for i in range(2):
+                ci[i, rows(at0), :] = jnp.zeros((8, L), jnp.int32)
+                for field in range(NF):
+                    a[field, i, rows(at0), :] = zero8
+            re[rows(at0), :] = zero8
+            rw[rows(at0), :] = zero8
 
     th_load.wait()
 
@@ -251,17 +285,18 @@
 
     ghosts = window(lane, 4, HALO) | window(lane, 119, HALO)
     ends = (0, R + 8)
-    for first_row in (0, 48, 96):
-        spots = [first_row + 8 * t for t in range(6)]
+
+    def unpack(spots, beneath):
         from_east = [re[rows(at), :] for at in spots]
         from_west = [rw[rows(at), :] for at in spots]
         for field, at, first, _ in PLAN:
             mask = window(lane, at, first)
             for j, spot in enumerate(spots):
                 value = turn(jnp.where(mask, from_east[j], from_west[j]), 4 - at)
-                if spot not in ends:
-                    value = jnp.where(ghosts, value, s[field, rows(spot), :])
-                s[field, rows(spot), :] = value
+                s[field, rows(spot), :] = jnp.where(ghosts, value, beneath(field, spot))
+
+    for first_row in (8, 72):
+        unpack([first_row + 8 * t for t in range(8)], lambda field, at: s[field, rows(at), :])
 
     def beside(tile):
         return turn(tile, 4), turn(tile, -4)
@@ -318,26 +353,12 @@
 
     lax.fori_loop(0, K // UNROLL, seams, 0)
 
-    wait_rows(sized(row_rows), recv_sem.at[1])
-
-    zero8 = jnp.zeros((8, L), f32)
+    each_end(recv_sem)
+
     for at in ends:
         for i in range(2):
             cf[i, rows(at), :] = ci[i, rows(at), :].astype(f32)
-
-    def shut():
-        for at0, edge in ((0, 0), (R + 8, ngy - 1)):
-
-            @pl.when(gy == edge)
-            def _(at0=at0):
-                cf[0, rows(at0), :] = zero8
-                cf[1, rows(at0), :] = zero8
-                s[CO, rows(at0), :] = zero8
-
-    for field in range(NF + 1):
-        for at in ends:
-            s[field, rows(at), :] = jnp.where(ghosts, s[field, rows(at), :], seam(field, at))
-    shut()
+    unpack(ends, seam)
 
     strips = (4, R + 4)
     for at in strips:
@@ -491,7 +512,8 @@
             h_out[rows(8 * t), halves[i]] = (
                 heights[0] * v0_s[i, rows(at), :] + heights[1] * v1_s[i, rows(at), :] + heights[2] * v2_s[i, rows(at), :])
 
-    wait_rows(sized(sent_rows), send_sem)
+    wait_rows(sized(column_rows), send_sem.at[0])
+    each_end(send_sem)
     for buf, n, i in reduce_sends:
         pltpu.make_async_copy(buf.at[pl.ds(0, n)], buf.at[pl.ds(0, n)], rs_sem.at[i]).wait()
 
@@ -545,8 +567,8 @@
             pltpu.VMEM((32, 1, L), f32),
             pltpu.VMEM((8, 1, L), f32),
             pltpu.SemaphoreType.DMA((K // PAIR + 2,)),
-            pltpu.SemaphoreType.DMA,
-            pltpu.SemaphoreType.DMA((2,)),
+            pltpu.SemaphoreType.DMA((3,)),
+            pltpu.SemaphoreType.DMA((3,)),
             pltpu.SemaphoreType.DMA((2,)),
             pltpu.SemaphoreType.DMA((2,)),
         ],

time: 29.1 us -> 28.7 us (0.986)
  Pallas kernels: 28.4 us -> 28 us
    pallas_call x1, Pallas kernels: 27.4 us -> 27 us  [on_device(): pl.pallas_call(functools.partial(kernel, ngy, ngx), out_shape=(pltpu.VMEM...]
where the time goes in v5:
time: 28.7 us; the launch traced here: 28.6 us
  Pallas kernels  28 us (98%)
  between operations  0.64 us (2%)
    pallas_call x1, Pallas kernels, on_device(): pl.pallas_call(functools.partial(kernel, ngy, ngx), out_shape=(pltpu.VMEM...  27 us
    pallas_call x1, Pallas kernels, on_device(): pl.pallas_call(put_kernel, out_shape=(jax.ShapeDtypeStruct((K, R, C), f32...  1.02 us

profile of v5, /device:TPU:1, one launch (start us, length us, event | category | flops | bytes accessed | tf_op | source)
XLA Modules:
  0.0 28.6 jit_solution(3770724050900774770)
XLA Ops:
  0.6 27.0 %shard_map.86 = (f32[8,128,256]{2,1,0:T(8,128)S(1)}, f32[128,256]{1,0:T(8,128)S(1)}) custom-call(f32[8,128,256]{2,1,0:T(8,128)} %tr_hbm.1, f32[8,128,256]{2,1,0:T(8,128)} %ea_hbm.1, f32[8,128,256]{2,1,0:T(8,128)} %no_hbm.1, s32[128,256]{1,0:T(8,128)} %co_hbm.1, f32[8]{0:T(128)} %th_hbm.1, f32[128,256]{1,0:T(8,128)} %sf_hbm.1, f32[128,256]{1,0:T(8,128)} %he_hbm.1), custom_call_target="tpu_custom_call" | custom-call | tf_op jit(solution)/shard_map/pallas_call | solution.py:533
  27.6 1.0 %shard_map.87 = (f32[8,128,256]{2,1,0:T(8,128)}, f32[128,256]{1,0:T(8,128)}) custom-call(f32[8,128,256]{2,1,0:T(8,128)S(1)} %get-tuple-element.4.tr, f32[128,256]{1,0:T(8,128)S(1)} %get-tuple-element.5.h), custom_call_target="tpu_custom_call" | custom-call | tf_op jit(solution)/shard_map/pallas_call | solution.py:577

commit v6 on v5

--- a/solution.py
+++ b/solution.py
@@ -15,22 +15,23 @@
 MESH = pl.DeviceIdType.MESH
 TR, EA, NO, SF, HE, CO = 0, K, 2 * K, 3 * K, 3 * K + 1, 3 * K + 2
 NF = 3 * K + 2
-UNROLL = 4
 STRIP_UNROLL = 8
 PAIR = 2
 
 
+SLOT = 32
+QUADS = 4
+STARTS = {TR: (0, 14), EA: (5, 19), NO: (9, 23)}
+WIDTHS = {TR: (5, 5), EA: (4, 5), NO: (4, 4)}
+PLANES = ((CO, 27, 4), (SF, 59, 3), (HE, 91, 3))
+S_SF, S_HE, S_CO = 6, 7, 8
+
+
 def lane_plan():
-    order = []
+    plan = [(field, at, width, width) for field, at, width in PLANES]
     for k in range(K):
-        order += [(TR + k, 5, 5), (EA + k, 4, 5), (NO + k, 4, 4)]
-    order += [(SF, 3, 3), (HE, 3, 3), (CO, 5, 5)]
-    plan, at = [], 0
-    for i, (field, first, last) in enumerate(order):
-        if i:
-            at += max(order[i - 1][1], last)
-        plan.append((field, at, first, last))
-    assert at + 5 <= L - 4
+        for base in (TR, EA, NO):
+            plan.append((base + k, SLOT * (k % QUADS) + STARTS[base][k // QUADS]) + WIDTHS[base])
     return plan
 
 
@@ -98,15 +99,15 @@
     greet(near)
     own, both = pl.ds(8, R), pl.ds(0, 2)
     halves = [pl.ds(0, L), pl.ds(L, L)]
+    for src, dst in ((sf_hbm, a.at[SF]), (he_hbm, a.at[HE]), (co_hbm, ci)):
+        for i, half in enumerate(halves):
+            pltpu.make_async_copy(src.at[:, half], dst.at[i, own], load_sem.at[K // PAIR]).start()
     for g in range(K // PAIR):
         for src, base in ((tr_hbm, TR), (ea_hbm, EA), (no_hbm, NO)):
             for i, half in enumerate(halves):
                 pltpu.make_async_copy(
                     src.at[pl.ds(PAIR * g, PAIR), :, half], a.at[pl.ds(base + PAIR * g, PAIR), i, own], load_sem.at[g]
                 ).start()
-    for src, dst in ((sf_hbm, a.at[SF]), (he_hbm, a.at[HE]), (co_hbm, ci)):
-        for i, half in enumerate(halves):
-            pltpu.make_async_copy(src.at[:, half], dst.at[i, own], load_sem.at[K // PAIR]).start()
     th_load = pltpu.make_async_copy(th_hbm, th, load_sem.at[K // PAIR + 1])
     th_load.start()
     greet(far1 + group2)
@@ -118,19 +119,29 @@
     tiles = range(R // 8)
 
     packs = [[jnp.zeros((8, L), f32) for _ in tiles] for _ in range(2)]
-    for g in range(K // PAIR + 1):
-        wait_rows(a.at[pl.ds(0, 3 * PAIR if g < K // PAIR else 3), both, own], load_sem.at[g])
-        for field, at, first, last in PLAN[3 * PAIR * g : 3 * PAIR * (g + 1)]:
+    for g in range(-1, K // PAIR):
+        wait_rows(a.at[pl.ds(0, 3 if g < 0 else 3 * PAIR), both, own], load_sem.at[g if g >= 0 else K // PAIR])
+        if g < 0:
+            for side in range(2):
+                for t in tiles:
+                    depth = ci[side, rows(8 + 8 * t), :].astype(f32)
+                    beyond = turn(depth, -1)
+                    if side:
+                        beyond = jnp.where(lane == L - 1, float(K), beyond)
+                    sh_s[0, side, rows(8 * t), :] = jnp.minimum(depth, beyond)
+        begin = 0 if g < 0 else 3 + 3 * PAIR * g
+        for field, at, first, last in PLAN[begin : begin + (3 if g < 0 else 3 * PAIR)]:
             for side in range(2):
                 width = last if side else first
-                start = at - 8 - width if side else at
-                mask = window(lane, start, width)
+                mask = window(lane, at - 8 - width if side else at, width)
                 shift = at - 8 if side else at
                 for t in tiles:
                     if field == CO:
                         value = ci[side, rows(8 + 8 * t), :].astype(f32)
                     else:
                         value = a[field, side, rows(8 + 8 * t), :]
+                    if EA <= field < NO:
+                        value = jnp.where(sh_s[0, side, rows(8 * t), :] > float(field - EA), value, 0.0)
                     packs[side][t] = jnp.where(mask, turn(value, shift), packs[side][t])
     for side, dest in enumerate((pw, pe)):
         for t in tiles:
@@ -208,6 +219,20 @@
             a[field, 0, rows(at), :], a[field, 1, rows(at), :])
         return jnp.where(lane < 64, turn(right, 4), turn(left, -4))
 
+    def seam_quad(base, half, at):
+        tile = jnp.zeros((8, L), f32)
+        for q in range(QUADS):
+            field = base + QUADS * half + q
+            tile = jnp.where(window(lane, SLOT * q, 4), turn(a[field, 1, rows(at), :], SLOT * q + 4), tile)
+            tile = jnp.where(window(lane, SLOT * q - 4, 4), turn(a[field, 0, rows(at), :], SLOT * q - 4), tile)
+        return tile
+
+    quads = [(base, half) for base in (TR, EA, NO) for half in range(2)]
+    planes = ((S_SF, SF), (S_HE, HE), (S_CO, CO))
+
+    def own_seam(tile, at):
+        return seam_quad(*quads[tile], at) if tile < 6 else seam(planes[tile - 6][1], at)
+
     def diagonal(i, at, helm, depth):
         inv_s[i, rows(at), :] = 1.0 / (6.0 + helm)
         wet_s[i, rows(at), :] = jnp.where(depth > 0.0, 1.0, 0.0)
@@ -218,9 +243,9 @@
             cf[i, rows(at), :] = ci[i, rows(at), :].astype(f32)
             fx[i, rows(at), :] = a[SF, i, rows(at), :]
             diagonal(i, at, a[HE, i, rows(at), :], cf[i, rows(at), :])
-    for field in range(NF + 1):
+    for tile in range(9):
         for t in tiles:
-            s[field, rows(8 + 8 * t), :] = seam(field, 8 + 8 * t)
+            s[tile, rows(8 + 8 * t), :] = own_seam(tile, 8 + 8 * t)
 
     def face_masks(at, below):
         depth = [cf[i, rows(at), :] for i in range(2)]
@@ -283,20 +308,38 @@
 
     wait_rows(sized(column_rows), recv_sem.at[0])
 
-    ghosts = window(lane, 4, HALO) | window(lane, 119, HALO)
+    within = lane & (SLOT - 1)
+    ghosts = ((within >= 4) & (within < 9)) | ((within >= 23) & (within < 28))
+    near_ghosts = window(lane, 4, 4) | window(lane, 120, 4)
+    outer_ghosts = window(lane, 8, 1) | window(lane, 119, 1)
+    own_lanes = window(lane, 124, 8)
     ends = (0, R + 8)
 
     def unpack(spots, beneath):
         from_east = [re[rows(at), :] for at in spots]
         from_west = [rw[rows(at), :] for at in spots]
-        for field, at, first, _ in PLAN:
-            mask = window(lane, at, first)
+        for tile in range(9):
+            if tile < 6:
+                base, half = quads[tile]
+                start = STARTS[base][half]
+                mask = ((lane - start) & (SLOT - 1)) < WIDTHS[base][0]
+            else:
+                start, width = {SF: (59, 3), HE: (91, 3), CO: (27, 4)}[planes[tile - 6][1]]
+                mask = window(lane, start, width)
             for j, spot in enumerate(spots):
-                value = turn(jnp.where(mask, from_east[j], from_west[j]), 4 - at)
-                s[field, rows(spot), :] = jnp.where(ghosts, value, beneath(field, spot))
+                value = turn(jnp.where(mask, from_east[j], from_west[j]), 4 - start)
+                below = beneath(tile, spot)
+                if tile == S_CO:
+                    value = jnp.where(near_ghosts, value, jnp.where(own_lanes, below, 0.0))
+                    value = jnp.where(outer_ghosts, float(K), value)
+                    value = value + turn(value, SLOT)
+                    value = value + turn(value, 2 * SLOT)
+                else:
+                    value = jnp.where(ghosts, value, below)
+                s[tile, rows(spot), :] = value
 
     for first_row in (8, 72):
-        unpack([first_row + 8 * t for t in range(8)], lambda field, at: s[field, rows(at), :])
+        unpack([first_row + 8 * t for t in range(8)], lambda tile, at: s[tile, rows(at), :])
 
     def beside(tile):
         return turn(tile, 4), turn(tile, -4)
@@ -307,58 +350,60 @@
 
     for t in tiles:
         at = 8 + 8 * t
-        depth = s[CO, rows(at), :]
+        depth = s[S_CO, rows(at), :]
         mes_s[rows(at), :] = jnp.minimum(depth, turn(depth, -1))
         below = min(at, R - 1)
-        mns_s[rows(below), :] = jnp.minimum(s[CO, rows(below), :], s[CO, rows(below + 1), :])
-        fs[rows(at), :] = s[SF, rows(at), :]
-        diagonal(2, at, ghost_tile(HE, at), ghost_tile(CO, at))
-
-    def seam_flux(k, kf, current, at):
-        speed = jnp.where(mns_s[rows(at), :] > kf, s[NO + k, rows(at), :], 0.0)
+        mns_s[rows(below), :] = jnp.minimum(s[S_CO, rows(below), :], s[S_CO, rows(below + 1), :])
+        fs[rows(at), :] = zero8
+        diagonal(2, at, ghost_tile(S_HE, at), ghost_tile(S_CO, at))
+
+    slot = ((lane + SLOT // 2) // SLOT) & (QUADS - 1)
+    floors = [(slot + QUADS * half).astype(f32) for half in range(2)]
+    weights = []
+    for half in range(2):
+        weight = jnp.zeros((8, L), f32)
+        for q in range(QUADS):
+            weight = jnp.where(slot == q, th[QUADS * half + q], weight)
+        weights.append(weight)
+
+    def seam_flux(half, current, at):
+        speed = jnp.where(mns_s[rows(at), :] > floors[half], s[4 + half, rows(at), :], 0.0)
         return speed * jnp.where(speed > 0.0, current(at), current(at + 1))
 
-    def seam_step(k, j, kf, current, store, starts, direct):
+    def seam_step(half, current, store, starts, direct):
         if not direct:
             for at in [at - 1 for at in starts] + [starts[-1]]:
-                fls[j, rows(at), :] = seam_flux(k, kf, current, at)
+                fls[half, rows(at), :] = seam_flux(half, current, at)
         for at in starts:
             now = current(at)
-            speed = jnp.where(mes_s[rows(at), :] > kf, s[EA + k, rows(at), :], 0.0)
+            speed = jnp.where(mes_s[rows(at), :] > floors[half], s[2 + half, rows(at), :], 0.0)
             fe = speed * jnp.where(speed > 0.0, now, turn(now, -1))
             if direct:
-                fn, fb = seam_flux(k, kf, current, at), seam_flux(k, kf, current, at - 1)
+                fn, fb = seam_flux(half, current, at), seam_flux(half, current, at - 1)
             else:
-                fn, fb = fls[j, rows(at), :], fls[j, rows(at - 1), :]
+                fn, fb = fls[half, rows(at), :], fls[half, rows(at - 1), :]
             store(at, now - (fe - turn(fe, 1) + fn - fb))
 
-    def seam_levels(k, j, starts1, starts2, direct):
-        kf = k.astype(f32)
-        weight = th[k]
-
+    def seam_levels(half, starts1, starts2, direct):
         def put1(at, value):
-            c1s[k, rows(at), :] = value
+            c1s[half, rows(at), :] = value
 
         def put2(at, value):
-            c2s[k, rows(at), :] = value
-            fs[rows(at), :] += jnp.where(s[CO, rows(at), :] > kf, weight * value, 0.0)
-
-        seam_step(k, j, kf, lambda at: s[TR + k, rows(at), :], put1, starts1, direct)
-        seam_step(k, j, kf, lambda at: c1s[k, rows(at), :], put2, starts2, direct)
-
-    def seams(step, carry):
-        for j in range(UNROLL):
-            seam_levels(step * UNROLL + j, j, starts1, starts2, False)
-        return carry
-
-    lax.fori_loop(0, K // UNROLL, seams, 0)
+            c2s[half, rows(at), :] = value
+            fs[rows(at), :] += jnp.where(s[S_CO, rows(at), :] > floors[half], weights[half] * value, 0.0)
+
+        seam_step(half, lambda at: s[half, rows(at), :], put1, starts1, direct)
+        seam_step(half, lambda at: c1s[half, rows(at), :], put2, starts2, direct)
+
+    for half in range(2):
+        seam_levels(half, starts1, starts2, False)
 
     each_end(recv_sem)
 
     for at in ends:
         for i in range(2):
             cf[i, rows(at), :] = ci[i, rows(at), :].astype(f32)
-    unpack(ends, seam)
+    unpack(ends, own_seam)
 
     strips = (4, R + 4)
     for at in strips:
@@ -367,30 +412,33 @@
         for i in range(2):
             mn_s[i, rows(below), :] = jnp.minimum(cf[i, rows(below), :], cf[i, rows(below + 1), :])
             fx[i, rows(at), :] = a[SF, i, rows(at), :]
-        depth = s[CO, rows(at), :]
+        depth = s[S_CO, rows(at), :]
         mes_s[rows(at), :] = jnp.minimum(depth, turn(depth, -1))
         for below in (at - 1, at + 1):
-            mns_s[rows(below), :] = jnp.minimum(s[CO, rows(below), :], s[CO, rows(below + 1), :])
-        fs[rows(at), :] = s[SF, rows(at), :]
+            mns_s[rows(below), :] = jnp.minimum(s[S_CO, rows(below), :], s[S_CO, rows(below + 1), :])
+        fs[rows(at), :] = zero8
     for at in ends:
         for i in range(2):
             diagonal(i, at, a[HE, i, rows(at), :], cf[i, rows(at), :])
-        diagonal(2, at, ghost_tile(HE, at), ghost_tile(CO, at))
+        diagonal(2, at, ghost_tile(S_HE, at), ghost_tile(S_CO, at))
 
     def edges(step, carry):
         for j in range(STRIP_UNROLL):
             k = step * STRIP_UNROLL + j
             own_levels(k, strips, strips, True)
-            seam_levels(k, j, strips, strips, True)
         return carry
 
+    for half in range(2):
+        seam_levels(half, strips, strips, True)
     lax.fori_loop(0, K // STRIP_UNROLL, edges, 0)
 
     blocks = [1] + [8 * t for t in range(1, 18)]
     inside = [8 * t for t in range(1, 17)]
 
     for at in blocks:
-        f_w, f_e = beside(fs[rows(at), :])
+        folded = fs[rows(at), :]
+        folded = folded + turn(folded, SLOT)
+        f_w, f_e = beside(folded + turn(folded, 2 * SLOT) + s[S_SF, rows(at), :])
         forcing = [
             jnp.where(lane < 2, f_w, fx[0, rows(at), :]),
             jnp.where(lane >= L - 2, f_e, fx[1, rows(at), :]),
@@ -446,15 +494,18 @@
     operator(2, v2_s, inside, store3)
 
     def finish_tracer():
-        def put(k, carry):
-            for t in tiles:
-                at = 8 + 8 * t
-                turned = beside(c2s[k, rows(at), :])
-                for i, mask in enumerate((lane < 2, lane >= L - 2)):
-                    tr_out[k, rows(8 * t), halves[i]] = jnp.where(mask, turned[i], c2[k, i, rows(at), :])
+        def put(half, carry):
+            for q in range(QUADS):
+                k = QUADS * half + q
+                for t in tiles:
+                    at = 8 + 8 * t
+                    patch = c2s[half, rows(at), :]
+                    patches = turn(patch, 4 - SLOT * q), turn(patch, -4 - SLOT * q)
+                    for i, mask in enumerate((lane < 2, lane >= L - 2)):
+                        tr_out[k, rows(8 * t), halves[i]] = jnp.where(mask, patches[i], c2[k, i, rows(at), :])
             return carry
 
-        lax.fori_loop(0, K, put, 0)
+        lax.fori_loop(0, K // QUADS, put, 0)
 
     lane1 = lax.broadcasted_iota(jnp.int32, (1, 128), 1)
     packed = jnp.zeros((1, 128), jnp.float32)
@@ -540,13 +591,13 @@
             pltpu.VMEM((NF, 2, RE, L), f32),
             pltpu.VMEM((2, RE, L), jnp.int32),
             pltpu.VMEM((2, RE, L), f32),
-            pltpu.VMEM((NF + 1, RE, L), f32),
+            pltpu.VMEM((9, RE, L), f32),
             pltpu.VMEM((K, 2, RE, L), f32),
             pltpu.VMEM((K, 2, RE, L), f32),
-            pltpu.VMEM((K, RE, L), f32),
-            pltpu.VMEM((K, RE, L), f32),
             pltpu.VMEM((2, RE, L), f32),
-            pltpu.VMEM((UNROLL, RE, L), f32),
+            pltpu.VMEM((2, RE, L), f32),
+            pltpu.VMEM((2, RE, L), f32),
+            pltpu.VMEM((2, RE, L), f32),
             pltpu.VMEM((2, RE, L), f32),
             pltpu.VMEM((2, RE, L), f32),
             pltpu.VMEM((RE, L), f32),

time: 28.7 us -> 28.2 us (0.983)
  Pallas kernels: 28 us -> 27.5 us
    pallas_call x1, Pallas kernels: 27 us -> 26.5 us  [on_device(): pl.pallas_call(functools.partial(kernel, ngy, ngx), out_shape=(pltpu.VMEM...]
where the time goes in v6:
time: 28.2 us; the launch traced here: 28.1 us
  Pallas kernels  27.5 us (98%)
  between operations  0.64 us (2%)
    pallas_call x1, Pallas kernels, on_device(): pl.pallas_call(functools.partial(kernel, ngy, ngx), out_shape=(pltpu.VMEM...  26.5 us
    pallas_call x1, Pallas kernels, on_device(): pl.pallas_call(put_kernel, out_shape=(jax.ShapeDtypeStruct((K, R, C), f32...  1.02 us

profile of v6, /device:TPU:1, one launch (start us, length us, event | category | flops | bytes accessed | tf_op | source)
XLA Modules:
  0.0 28.1 jit_solution(9462702214399900366)
XLA Ops:
  0.6 26.5 %shard_map.86 = (f32[8,128,256]{2,1,0:T(8,128)S(1)}, f32[128,256]{1,0:T(8,128)S(1)}) custom-call(f32[8,128,256]{2,1,0:T(8,128)} %tr_hbm.1, f32[8,128,256]{2,1,0:T(8,128)} %ea_hbm.1, f32[8,128,256]{2,1,0:T(8,128)} %no_hbm.1, s32[128,256]{1,0:T(8,128)} %co_hbm.1, f32[8]{0:T(128)} %th_hbm.1, f32[128,256]{1,0:T(8,128)} %sf_hbm.1, f32[128,256]{1,0:T(8,128)} %he_hbm.1), custom_call_target="tpu_custom_call" | custom-call | tf_op jit(solution)/shard_map/pallas_call | solution.py:584
  27.1 1.0 %shard_map.87 = (f32[8,128,256]{2,1,0:T(8,128)}, f32[128,256]{1,0:T(8,128)}) custom-call(f32[8,128,256]{2,1,0:T(8,128)S(1)} %get-tuple-element.4.tr, f32[128,256]{1,0:T(8,128)S(1)} %get-tuple-element.5.h), custom_call_target="tpu_custom_call" | custom-call | tf_op jit(solution)/shard_map/pallas_call | solution.py:628

commit v7 on v6

--- a/solution.py
+++ b/solution.py
@@ -12,10 +12,10 @@
 R, C, L = 128, 256, 128
 RE = R + 24
 HALO = 5
+SHIFT = 0.75
 MESH = pl.DeviceIdType.MESH
 TR, EA, NO, SF, HE, CO = 0, K, 2 * K, 3 * K, 3 * K + 1, 3 * K + 2
 NF = 3 * K + 2
-STRIP_UNROLL = 8
 PAIR = 2
 
 
@@ -85,7 +85,11 @@
         (lax.rem(gy + dy, ngy), lax.rem(gx + 8 * dh, ngx))
         for dh in range(2) for dy in range(16) if dy or dh
     ]
-    far1 = [device for i, device in enumerate(group1) if i not in (0, 14)]
+    def far_first(entry):
+        dy, dh = (entry[0] + 1) % 16, (entry[0] + 1) // 16
+        return -2 * dh - min(dy % 8, 8 - dy % 8)
+
+    far1 = [device for i, device in sorted(enumerate(group1), key=far_first) if i not in (0, 14)]
     group2 = [(gy, hi * 8 + lax.rem(z + dz, 8)) for dz in range(1, 8)]
     near = [(north, gx), (south, gx), (gy, e_id), (gy, w_id),
             (north, e_id), (north, w_id), (south, e_id), (south, w_id)]
@@ -102,6 +106,7 @@
     for src, dst in ((sf_hbm, a.at[SF]), (he_hbm, a.at[HE]), (co_hbm, ci)):
         for i, half in enumerate(halves):
             pltpu.make_async_copy(src.at[:, half], dst.at[i, own], load_sem.at[K // PAIR]).start()
+    greet(far1 + group2)
     for g in range(K // PAIR):
         for src, base in ((tr_hbm, TR), (ea_hbm, EA), (no_hbm, NO)):
             for i, half in enumerate(halves):
@@ -110,7 +115,6 @@
                 ).start()
     th_load = pltpu.make_async_copy(th_hbm, th, load_sem.at[K // PAIR + 1])
     th_load.start()
-    greet(far1 + group2)
 
     def wait_rows(ref, sem):
         pltpu.make_async_copy(ref, ref, sem).wait()
@@ -284,7 +288,7 @@
                 store(i, at, now[i] - (fe[i] - fw[i] + fn - fb))
 
     def own_levels(k, starts1, starts2, direct):
-        kf = k.astype(f32)
+        kf = float(k) if isinstance(k, int) else k.astype(f32)
         weight = th[k]
 
         def put1(i, at, value):
@@ -332,8 +336,7 @@
                 if tile == S_CO:
                     value = jnp.where(near_ghosts, value, jnp.where(own_lanes, below, 0.0))
                     value = jnp.where(outer_ghosts, float(K), value)
-                    value = value + turn(value, SLOT)
-                    value = value + turn(value, 2 * SLOT)
+                    value = value + turn(value, SLOT) + turn(value, 2 * SLOT) + turn(value, 3 * SLOT)
                 else:
                     value = jnp.where(ghosts, value, below)
                 s[tile, rows(spot), :] = value
@@ -422,23 +425,18 @@
             diagonal(i, at, a[HE, i, rows(at), :], cf[i, rows(at), :])
         diagonal(2, at, ghost_tile(S_HE, at), ghost_tile(S_CO, at))
 
-    def edges(step, carry):
-        for j in range(STRIP_UNROLL):
-            k = step * STRIP_UNROLL + j
-            own_levels(k, strips, strips, True)
-        return carry
-
     for half in range(2):
         seam_levels(half, strips, strips, True)
-    lax.fori_loop(0, K // STRIP_UNROLL, edges, 0)
+    for k in range(K):
+        own_levels(k, strips, strips, True)
 
     blocks = [1] + [8 * t for t in range(1, 18)]
     inside = [8 * t for t in range(1, 17)]
 
     for at in blocks:
         folded = fs[rows(at), :]
-        folded = folded + turn(folded, SLOT)
-        f_w, f_e = beside(folded + turn(folded, 2 * SLOT) + s[S_SF, rows(at), :])
+        folded = folded + turn(folded, SLOT) + turn(folded, 2 * SLOT) + turn(folded, 3 * SLOT)
+        f_w, f_e = beside(folded + s[S_SF, rows(at), :])
         forcing = [
             jnp.where(lane < 2, f_w, fx[0, rows(at), :]),
             jnp.where(lane >= L - 2, f_e, fx[1, rows(at), :]),
@@ -453,9 +451,7 @@
     def operator(n, src, spots, store):
         spread = {}
         for at in blocks:
-            w = [src[i, rows(at), :] for i in range(3)]
-            if n == 0:
-                w = [wet_s[i, rows(at), :] * w[i] for i in range(3)]
+            w = [wet_s[i, rows(at), :] * src[i, rows(at), :] for i in range(3)]
             h = [x + y for x, y in zip(ring_west(w, lane), ring_east(w, lane))]
             spread[at] = h
             for i in range(3):
@@ -470,24 +466,28 @@
         return i < 2 and at in inside
 
     def store1(i, at, u):
-        v = u * inv_s[i, rows(at), :]
+        f = fx[i, rows(at), :]
+        g = u - SHIFT * f
+        v = g * inv_s[i, rows(at), :]
         v1_s[i, rows(at), :] = v
+        sh_s[2, i, rows(at), :] = g
         if counted(i, at):
-            f = fx[i, rows(at), :]
             nu[0][i] += f * v0_s[i, rows(at), :]
             nu[1][i] += v * f
-            nu[2][i] += v * u
+            nu[2][i] += v * g
 
     def store2(i, at, u):
-        v = u * inv_s[i, rows(at), :]
+        g = u - SHIFT * sh_s[2, i, rows(at), :]
+        v = g * inv_s[i, rows(at), :]
         v2_s[i, rows(at), :] = v
+        sh_s[0, i, rows(at), :] = g
         if counted(i, at):
-            nu[3][i] += v1_s[i, rows(at), :] * u
-            nu[4][i] += v * u
+            nu[3][i] += v1_s[i, rows(at), :] * g
+            nu[4][i] += v * g
 
     def store3(i, at, u):
         if counted(i, at):
-            nu[5][i] += v2_s[i, rows(at), :] * u
+            nu[5][i] += v2_s[i, rows(at), :] * (u - SHIFT * sh_s[0, i, rows(at), :])
 
     operator(0, v0_s, blocks, store1)
     operator(1, v1_s, blocks, store2)
@@ -541,7 +541,7 @@
                 total = term if total is None else total + term
         return total
 
-    diff = [m[i] - m[i + 1] for i in range(5)]
+    diff = [(1.0 - SHIFT) * m[i] - m[i + 1] for i in range(5)]
     one = jnp.ones_like(m[0])
     zc, pc = [one], [one]
     heights = [jnp.zeros_like(one)] * 3
@@ -550,7 +550,7 @@
         alpha = rz / form(pc, diff)
         heights = [h + alpha * pc[i] if i < len(pc) else h for i, h in enumerate(heights)]
         if it + 1 < ITERS:
-            applied = [p - q for p, q in zip(pc + [jnp.zeros_like(one)], [jnp.zeros_like(one)] + pc)]
+            applied = [(1.0 - SHIFT) * p - q for p, q in zip(pc + [jnp.zeros_like(one)], [jnp.zeros_like(one)] + pc)]
             zc = [(zc[i] if i < len(zc) else 0.0) - alpha * applied[i] for i in range(len(applied))]
             rz_next = form(zc, m)
             beta = rz_next / rz

time: 28.2 us -> 28.2 us (level)
  no operation moved by 1% of the time
where the time goes in v7:
time: 28.2 us; the launch traced here: 28 us
  Pallas kernels  27.4 us (97%)
  between operations  0.64 us (2%)
    pallas_call x1, Pallas kernels, on_device(): pl.pallas_call(functools.partial(kernel, ngy, ngx), out_shape=(pltpu.VMEM...  26.4 us
    pallas_call x1, Pallas kernels, on_device(): pl.pallas_call(put_kernel, out_shape=(jax.ShapeDtypeStruct((K, R, C), f32...  1.02 us

profile of v7, /device:TPU:1, one launch (start us, length us, event | category | flops | bytes accessed | tf_op | source)
XLA Modules:
  0.0 28.0 jit_solution(18334218728719814411)
XLA Ops:
  0.6 26.4 %shard_map.86 = (f32[8,128,256]{2,1,0:T(8,128)S(1)}, f32[128,256]{1,0:T(8,128)S(1)}) custom-call(f32[8,128,256]{2,1,0:T(8,128)} %tr_hbm.1, f32[8,128,256]{2,1,0:T(8,128)} %ea_hbm.1, f32[8,128,256]{2,1,0:T(8,128)} %no_hbm.1, s32[128,256]{1,0:T(8,128)} %co_hbm.1, f32[8]{0:T(128)} %th_hbm.1, f32[128,256]{1,0:T(8,128)} %sf_hbm.1, f32[128,256]{1,0:T(8,128)} %he_hbm.1), custom_call_target="tpu_custom_call" | custom-call | tf_op jit(solution)/shard_map/pallas_call | solution.py:584
  27.0 1.0 %shard_map.87 = (f32[8,128,256]{2,1,0:T(8,128)}, f32[128,256]{1,0:T(8,128)}) custom-call(f32[8,128,256]{2,1,0:T(8,128)S(1)} %get-tuple-element.4.tr, f32[128,256]{1,0:T(8,128)S(1)} %get-tuple-element.5.h), custom_call_target="tpu_custom_call" | custom-call | tf_op jit(solution)/shard_map/pallas_call | solution.py:628
